TPU v7x, 256 devices: a whole 4x4x8 slice. The times are simulated.
256 devices in a mesh: row: 16 (over y, z_hi), col: 16 (over x, z_lo, core).
Axes of the slice: x: 4, y: 4, z: 8 (z_hi: 4, z_lo: 2; z = z_hi * 2 + z_lo), core: 2. Of those that a mesh axis runs over, the one named last changes fastest.
Arguments:
- rep_a: bfloat16 [8192, 512], P(('row', 'col')), may hold values from -100 to 100
- val_a: bfloat16 [8192, 512], P(('row', 'col')), may hold values from -6 to 6
- rep_b: bfloat16 [16384, 512], P(('row', 'col')), may hold values from -18 to 18
- val_b: bfloat16 [16384, 512], P(('row', 'col')), may hold values from -6 to 6
Outputs:
- mixed_a: float32 [8192, 512], P(('row', 'col'))
- mixed_b: float32 [16384, 512], P(('row', 'col'))
All inputs are finite; a program needn't handle non-finite values.
Results may differ from a plain program's by a relative error of at most 0.0015.
Values may be sent and summed in bfloat16 or wider, within the bound.
No kernel may reach another device: no remote copies, remote signals or barrier semaphores. Data moves between devices by JAX's collectives and lax.ppermute only.
A program may use at most 64 MiB of HBM per device.

v0:
```python
import functools

import jax
import jax.numpy as jnp
from jax import lax
from jax.experimental import pallas as pl
from jax.experimental.pallas import tpu as pltpu
from jax.sharding import Mesh
from jax.sharding import PartitionSpec as P


HEADS = 4
HEAD = 128
SCALE = HEAD**-0.5 * 1.4426950408889634
LANES = 128
STATS = 16
AXES = ("y", "z2", "z1", "x", "z0", "core")
HEAD_AXIS, B_AXIS, A_FAR, A_NEAR, CORE = ("z2", "z1"), ("x",), ("y",), ("z0",), ("core",)
VMEM = pl.BlockSpec(memory_space=pltpu.VMEM)
SMEM = pl.BlockSpec(memory_space=pltpu.SMEM)
HBM = pl.BlockSpec(memory_space=pltpu.HBM)
GROUP = 256
PARAMS = pltpu.CompilerParams(vmem_limit_bytes=24 * 1024 * 1024)
SMALL = pltpu.CompilerParams(vmem_limit_bytes=8 * 1024 * 1024)

WIDE = pltpu.CompilerParams(vmem_limit_bytes=62 * 1024 * 1024)


def swap(value, axes, k):
    size = lax.axis_size(axes)
    return lax.ppermute(value, axes, [(i, i ^ k) for i in range(size)])


def exchange(blocks, axes):
    return [blocks[0]] + [swap(b, axes, k) for k, b in enumerate(blocks) if k]


def gather(block, axes):
    return exchange([block] * lax.axis_size(axes), axes)


def split_heads(place, *refs):
    sources, outs, sems = refs[:4], refs[4:-1], refs[-1]
    copies = []
    for k, out in enumerate(outs):
        lanes = pl.ds(pl.multiple_of((place[0] ^ k) * HEAD, HEAD), HEAD)
        at = 0
        for source in sources:
            rows = source.shape[0]
            copies.append(
                pltpu.make_async_copy(source.at[:, lanes], out.at[at : at + rows], sems.at[len(copies)])
            )
            at += rows
    for copy in copies:
        copy.start()
    for copy in copies:
        copy.wait()


def join_heads(place, *refs):
    blocks, (out_a, out_b) = refs[:-2], refs[-2:]
    rows_a = out_a.shape[0]
    for k, block in enumerate(blocks):
        lanes = pl.ds(pl.multiple_of((place[0] ^ k) * HEAD, HEAD), HEAD)
        out_a[:, lanes] = block[:rows_a, :]
        out_b[:, lanes] = block[rows_a:, :]


def packed(rows):
    return rows + STATS * (rows // LANES)


def stat_rows(level):
    line = jnp.transpose(level)[:STATS, :]
    first = line.astype(jnp.bfloat16).astype(jnp.float32)
    second = (line - first).astype(jnp.bfloat16).astype(jnp.float32)
    third = line - first - second
    row = lax.broadcasted_iota(jnp.int32, (STATS, LANES), 0)
    return jnp.where(row == 0, first, jnp.where(row == 1, second, jnp.where(row == 2, third, 0.0)))


def joined(parts):
    return parts[0] if len(parts) == 1 else jnp.concatenate(parts)


def attend_kernel(rows, span, n_q, n_kv, carried, final, *refs):
    q_refs, kv_refs = refs[:n_q], refs[n_q : n_q + n_kv]
    before = refs[n_q + n_kv : n_q + n_kv + 2 * carried]
    outs, scores = refs[n_q + n_kv + 2 * carried : -1], refs[-1]
    keys = [(ref, at) for ref in kv_refs for at in range(0, ref.shape[0], 2 * span)]
    blocks = [(i, j) for i, ref in enumerate(q_refs) for j in range(ref.shape[0] // (2 * rows))]
    step = GROUP // rows
    for g in range(0, len(blocks), step):
        group = blocks[g : g + step]
        size = rows * len(group)
        queries = joined([q_refs[i][2 * rows * j : 2 * rows * j + rows, :] for i, j in group])
        top = None
        for n, (ref, at) in enumerate(keys):
            logits = lax.dot_general(
                queries, ref[at : at + span, :], (((1,), (1,)), ((), ())), preferred_element_type=jnp.float32
            )
            scores[:size, n * span : (n + 1) * span] = logits
            for c in range(0, span, LANES):
                part = logits[:, c : c + LANES]
                top = part if top is None else jnp.maximum(top, part)
        peak = jnp.max(top, axis=1, keepdims=True) * SCALE
        total, number = None, None
        for n, (ref, at) in enumerate(keys):
            weights = jnp.exp2(scores[:size, n * span : (n + 1) * span] * SCALE - peak)
            for c in range(0, span, LANES):
                part = weights[:, c : c + LANES]
                total = part if total is None else total + part
            part = jnp.dot(
                weights.astype(jnp.bfloat16), ref[at + span : at + 2 * span, :], preferred_element_type=jnp.float32
            )
            number = part if number is None else number + part
        total = jnp.sum(total, axis=1, keepdims=True)
        mean = number / total
        level = jnp.broadcast_to(peak + jnp.log2(total), (size, LANES))
        where = slice(g * rows, g * rows + size)
        if carried:
            old_mean, old_level = before[0][where, :], before[1][where, :]
            best = jnp.maximum(level, old_level)
            new, old = jnp.exp2(level - best), jnp.exp2(old_level - best)
            mean = (mean * new + old_mean * old) / (new + old)
            level = best + jnp.log2(new + old)
        if not final:
            outs[0][where, :] = mean
            outs[1][where, :] = level
            continue
        for n, (i, j) in enumerate(group):
            at = j * packed(rows)
            outs[i][at : at + rows, :] = mean[n * rows : (n + 1) * rows, :]
            for c in range(rows // LANES):
                begin = n * rows + c * LANES
                outs[i][at + rows + c * STATS : at + rows + (c + 1) * STATS, :] = stat_rows(
                    level[begin : begin + LANES, :]
                )


def attention(rows, q_blocks, span, kv_stacks, before=(), final=True):
    heights = [q.shape[0] // 2 for q in q_blocks]
    whole = sum(heights)
    keys = sum(s.shape[0] for s in kv_stacks) // 2
    if final:
        shapes = [(h // rows * packed(rows), HEAD) for h in heights]
    else:
        shapes = [(whole, HEAD), (whole, LANES)]
    n_q, n_kv = len(q_blocks), len(kv_stacks)
    return pl.pallas_call(
        functools.partial(attend_kernel, rows, span, n_q, n_kv, len(before) // 2, final),
        out_shape=[jax.ShapeDtypeStruct(s, jnp.float32) for s in shapes],
        in_specs=[VMEM] * (n_q + n_kv + len(before)),
        out_specs=[VMEM] * len(shapes),
        scratch_shapes=[pltpu.VMEM((GROUP, keys), jnp.float32)],
        compiler_params=PARAMS,
        cost_estimate=pl.CostEstimate(flops=4 * whole * keys * HEAD, bytes_accessed=0, transcendentals=whole * keys),
    )(*q_blocks, *kv_stacks, *before)


def merged(refs, rows):
    parts = [r.at[: packed(rows)] for r in refs]
    columns = []
    for c in range(rows // LANES):
        at = rows + c * STATS
        levels = [jnp.sum(p[at : at + STATS, :], axis=0, keepdims=True) for p in parts]
        top = functools.reduce(jnp.maximum, levels)
        shares = [jnp.exp2(level - top) for level in levels]
        whole = functools.reduce(jnp.add, shares)
        result = None
        for part, share in zip(parts, shares):
            scale = jnp.transpose(jnp.broadcast_to(share / whole, (LANES, LANES)))
            term = part[c * LANES : (c + 1) * LANES, :] * scale
            result = term if result is None else result + term
        columns.append(result)
    return columns


def fold_kernel(rows, *refs):
    parts, out = refs[:-1], refs[-1]
    halves = [p.at[packed(rows) :] for p in parts]
    levels = [jnp.sum(h[rows : rows + STATS, :], axis=0, keepdims=True) for h in halves]
    top = functools.reduce(jnp.maximum, levels)
    shares = [jnp.exp2(level - top) for level in levels]
    whole = functools.reduce(jnp.add, shares)
    result = None
    for half, share in zip(halves, shares):
        term = half[:rows, :] * jnp.transpose(jnp.broadcast_to(share / whole, (LANES, LANES)))
        result = term if result is None else result + term
    out[:rows, :] = result
    out[rows:, :] = stat_rows(jnp.transpose(jnp.broadcast_to(top + jnp.log2(whole), (LANES, LANES))))


def merge_kernel(n_a, n_b, rows_of, *refs):
    parts_a, parts_b, outs = refs[:n_a], refs[n_a : n_a + n_b], refs[n_a + n_b :]
    at = 0
    for parts, rows in zip((parts_a, parts_b), rows_of):
        whole = merged(parts, rows)
        each = rows // len(outs)
        for k, out in enumerate(outs):
            column, offset = divmod(k * each, LANES)
            out[at : at + each, :] = whole[column][offset : offset + each, :]
        at += each


def both_ways(rep_a, val_a, rep_b, val_b):
    rows_a, rows_b = rep_a.shape[0], rep_b.shape[0]
    heads = lax.axis_size(HEAD_AXIS)
    place = lax.axis_index(HEAD_AXIS).astype(jnp.int32).reshape(1)
    bf16, f16, f32 = jnp.bfloat16, jnp.float16, jnp.float32

    message = jax.ShapeDtypeStruct((2 * (rows_a + rows_b), HEAD), bf16)
    sent = pl.pallas_call(
        split_heads,
        out_shape=[message] * heads,
        in_specs=[SMEM] + [HBM] * 4,
        out_specs=[VMEM] * heads,
        scratch_shapes=[pltpu.SemaphoreType.DMA((4 * heads,))],
        compiler_params=WIDE,
    )(place, rep_a, val_a, rep_b, val_b)
    took = exchange(sent, HEAD_AXIS)
    edges = (0, rows_a, 2 * rows_a, 2 * rows_a + rows_b, 2 * (rows_a + rows_b))
    own_a = jnp.concatenate([t[edges[i] : edges[i + 1]] for i in (0, 1) for t in took])
    own_b = jnp.concatenate([t[edges[i] : edges[i + 1]] for i in (2, 3) for t in took])
    span_a, span_b = heads * rows_a, heads * rows_b

    near_a = swap(own_a, A_NEAR, 1)
    blocks_b = gather(own_b, B_AXIS)
    pair_a = jnp.concatenate([own_a, near_a])
    pairs_a = gather(pair_a, A_FAR)
    all_b = jnp.concatenate(blocks_b)
    other_b = swap(all_b, CORE, 1)
    first_a = swap(pair_a, CORE, 1)
    rest_a = jnp.concatenate(pairs_a[1:])
    other_a = swap(rest_a, CORE, 1)

    keys_b = [all_b, other_b]
    part_a = attention(span_a, pairs_a[:1], span_b, keys_b)
    begun = attention(span_b, blocks_b, span_a, [pair_a, first_a], final=False)
    part_a += attention(span_a, pairs_a[1:], span_b, keys_b)
    part_a = [p.astype(f16) for p in part_a]
    part_a, other_a = lax.optimization_barrier((part_a, other_a))
    part_b = attention(span_b, blocks_b, span_a, [rest_a, other_a], before=begun)

    part_a = exchange(part_a, A_FAR)
    part_a = [p.astype(f32) for p in part_a]
    folded = pl.pallas_call(
        functools.partial(fold_kernel, span_a),
        out_shape=jax.ShapeDtypeStruct((packed(span_a), HEAD), f32),
        in_specs=[VMEM] * len(part_a),
        out_specs=VMEM,
        compiler_params=SMALL,
    )(*part_a)
    near_back = swap(folded.astype(f16), A_NEAR, 1)
    part_a = part_a + [near_back.astype(f32)]
    part_b = exchange([p.astype(f16) for p in part_b], B_AXIS)
    part_b = [p.astype(f32) for p in part_b]

    result = jax.ShapeDtypeStruct((rows_a + rows_b, HEAD), f32)
    done = pl.pallas_call(
        functools.partial(merge_kernel, len(part_a), len(part_b), (span_a, span_b)),
        out_shape=[result] * heads,
        in_specs=[VMEM] * (len(part_a) + len(part_b)),
        out_specs=[VMEM] * heads,
        compiler_params=SMALL,
    )(*part_a, *part_b)
    back = [done[0]] + [b.astype(f32) for b in exchange([d.astype(f16) for d in done], HEAD_AXIS)[1:]]
    return pl.pallas_call(
        join_heads,
        out_shape=[
            jax.ShapeDtypeStruct((rows_a, HEADS * HEAD), f32),
            jax.ShapeDtypeStruct((rows_b, HEADS * HEAD), f32),
        ],
        in_specs=[SMEM] + [VMEM] * heads,
        out_specs=[VMEM] * 2,
        compiler_params=SMALL,
    )(place, *back)


def solution(mesh):
    torus = Mesh(mesh.devices.reshape(4, 2, 2, 4, 2, 2), AXES)
    placed = P(AXES, None)
    return jax.shard_map(
        both_ways,
        mesh=torus,
        in_specs=(placed,) * 4,
        out_specs=(placed, placed),
        check_vma=False,
    )
```

profile of v0, /device:TPU:4, one launch (start us, length us, event | category | flops | bytes accessed | tf_op | source)
XLA Modules:
  0.0 70.4 jit_solution(13165110587133322114)
XLA Ops:
  0.6 1.7 %shard_map.59 = (bf16[192,128]{1,0:T(8,128)(2,1)}, bf16[192,128]{1,0:T(8,128)(2,1)}, bf16[192,128]{1,0:T(8,128)(2,1)}, bf16[192,128]{1,0:T(8,128)(2,1)}) custom-call(s32[1]{0:T(128)} %bitcast.place, bf16[32,512]{1,0:T(8,128)(2,1)} %refs_0_.1, bf16[32,512]{1,0:T(8,128)(2,1)} %refs_1_.1, bf16[64,512]{1,0:T(8,128)(2,1)} %refs_2_.1, bf16[64,512]{1,0:T(8,128)(2,1)} %refs_3_.1), custom_call_target="tpu_custom_call" | custom-call | tf_op jit(solution)/shard_map/pallas_call | solution.py:213
  2.3 3.4 %collective-permute-start = (bf16[192,128]{1,0:T(8,128)(2,1)}, bf16[192,128]{1,0:T(8,128)(2,1)S(1)}, u32[]{:S(2)}, u32[]{:S(2)}) collective-permute-start(bf16[192,128]{1,0:T(8,128)(2,1)} %get-tuple-element.25), channel_id=1, source_target_pairs={{0,16},{16,0},{32,48},{48,32},{1,17},{17,1},{33,49},{49,33},{2,18}... | collective-permute-start | bytes 147464 | tf_op jit(solution)/shard_map/ppermute | solution.py:31
  5.7 5.4 %collective-permute-start.1 = (bf16[192,128]{1,0:T(8,128)(2,1)}, bf16[192,128]{1,0:T(8,128)(2,1)S(1)}, u32[]{:S(2)}, u32[]{:S(2)}) collective-permute-start(bf16[192,128]{1,0:T(8,128)(2,1)} %get-tuple-element.26), channel_id=1, source_target_pairs={{0,32},{16,48},{32,0},{48,16},{1,33},{17,49},{33,1},{49,17},{2,34}... | collective-permute-start | bytes 147464 | tf_op jit(solution)/shard_map/ppermute | solution.py:31
  11.1 0.7 %constant_dynamic-update-slice_fusion.24 = bf16[512,128]{1,0:T(8,128)(2,1)S(1)} fusion(bf16[192,128]{1,0:T(8,128)(2,1)} %get-tuple-element.24), kind=kLoop, calls=%fused_computation.24 | loop fusion | bytes 32768
  11.8 0.7 constant_dynamic-update-slice_fusion.7
  12.5 1.4 %collective-permute-done.1 = bf16[192,128]{1,0:T(8,128)(2,1)S(1)} collective-permute-done((bf16[192,128]{1,0:T(8,128)(2,1)}, bf16[192,128]{1,0:T(8,128)(2,1)S(1)}, u32[]{:S(2)}, u32[]{:S(2)}) %collective-permute-start.1) | collective-permute-done | bytes 49184 | tf_op jit(solution)/shard_map/ppermute | solution.py:31
  13.9 3.7 %collective-permute-done.2 = bf16[192,128]{1,0:T(8,128)(2,1)S(1)} collective-permute-done((bf16[192,128]{1,0:T(8,128)(2,1)}, bf16[192,128]{1,0:T(8,128)(2,1)S(1)}, u32[]{:S(2)}, u32[]{:S(2)}) %collective-permute-start.2) | collective-permute-done | bytes 49184 | tf_op jit(solution)/shard_map/ppermute | solution.py:31
  18.3 2.7 %collective-permute-start.5 = (bf16[512,128]{1,0:T(8,128)(2,1)S(1)}, bf16[512,128]{1,0:T(8,128)(2,1)S(1)}, u32[]{:S(2)}, u32[]{:S(2)}) collective-permute-start(bf16[512,128]{1,0:T(8,128)(2,1)S(1)} %get-tuple-element.46.refs_0_), channel_id=1, source_target_pairs={{0,8},{4,12},{8,0},{12,4},{1,9},{5,13},{9,1},{13,5},{2,10},{6,14},... | collective-permute-start | bytes 393224 | tf_op jit(solution)/shard_map/ppermute | solution.py:31
  21.0 0.8 %collective-permute-start.4 = (bf16[512,128]{1,0:T(8,128)(2,1)S(1)}, bf16[512,128]{1,0:T(8,128)(2,1)S(1)}, u32[]{:S(2)}, u32[]{:S(2)}) collective-permute-start(bf16[512,128]{1,0:T(8,128)(2,1)S(1)} %get-tuple-element.46.refs_0_), channel_id=1, source_target_pairs={{0,4},{4,0},{8,12},{12,8},{1,5},{5,1},{9,13},{13,9},{2,6},{6,2},{1... | collective-permute-start | bytes 393224 | tf_op jit(solution)/shard_map/ppermute | solution.py:31
  21.9 1.0 %collective-permute-start.3 = (bf16[256,128]{1,0:T(8,128)(2,1)S(1)}, bf16[256,128]{1,0:T(8,128)(2,1)S(1)}, u32[]{:S(2)}, u32[]{:S(2)}) collective-permute-start(bf16[256,128]{1,0:T(8,128)(2,1)S(1)} %get-tuple-element.54), channel_id=1, source_target_pairs={{0,2},{2,0},{1,3},{3,1},{4,6},{6,4},{5,7},{7,5},{8,10},{10,8},{9,1... | collective-permute-start | bytes 196616 | tf_op jit(solution)/shard_map/ppermute | solution.py:31
  23.0 3.2 %collective-permute-done.3 = bf16[256,128]{1,0:T(8,128)(2,1)S(1)} collective-permute-done((bf16[256,128]{1,0:T(8,128)(2,1)S(1)}, bf16[256,128]{1,0:T(8,128)(2,1)S(1)}, u32[]{:S(2)}, u32[]{:S(2)}) %collective-permute-start.3) | collective-permute-done | bytes 65568 | tf_op jit(solution)/shard_map/ppermute | solution.py:31
  26.3 3.1 %collective-permute-start.10 = (bf16[512,128]{1,0:T(8,128)(2,1)S(1)}, bf16[512,128]{1,0:T(8,128)(2,1)S(1)}, u32[]{:S(2)}, u32[]{:S(2)}) collective-permute-start(bf16[512,128]{1,0:T(8,128)(2,1)S(1)} %constant_dynamic-update-slice_fusion.8.refs_0_.refs_4_), channel_id=1, source_target_pairs={{0,192},{64,128},{128,64},{192,0},{1,193},{65,129},{129,65},{193,1... | collective-permute-start | bytes 393224 | tf_op jit(solution)/shard_map/ppermute | solution.py:31
  30.6 4.3 %collective-permute-done.8.refs_0_ = bf16[512,128]{1,0:T(8,128)(2,1)S(1)} collective-permute-done((bf16[512,128]{1,0:T(8,128)(2,1)S(1)}, bf16[512,128]{1,0:T(8,128)(2,1)S(1)}, u32[]{:S(2)}, u32[]{:S(2)}) %collective-permute-start.8) | collective-permute-done | bytes 131104 | tf_op jit(solution)/shard_map/ppermute | solution.py:31
  35.0 0.9 %collective-permute-done.9.refs_1_ = bf16[512,128]{1,0:T(8,128)(2,1)S(1)} collective-permute-done((bf16[512,128]{1,0:T(8,128)(2,1)S(1)}, bf16[512,128]{1,0:T(8,128)(2,1)S(1)}, u32[]{:S(2)}, u32[]{:S(2)}) %collective-permute-start.9) | collective-permute-done | bytes 131104 | tf_op jit(solution)/shard_map/ppermute | solution.py:31
  36.5 1.4 %collective-permute-done.16.refs_5_ = bf16[512,128]{1,0:T(8,128)(2,1)S(1)} collective-permute-done((bf16[512,128]{1,0:T(8,128)(2,1)S(1)}, bf16[512,128]{1,0:T(8,128)(2,1)S(1)}, u32[]{:S(2)}, u32[]{:S(2)}) %collective-permute-start.16) | collective-permute-done | bytes 131104 | tf_op jit(solution)/shard_map/ppermute | solution.py:31
  37.9 1.2 %shard_map.63 = (f32[1024,128]{1,0:T(8,128)S(1)}, f32[1024,128]{1,0:T(8,128)S(1)}) custom-call(bf16[512,128]{1,0:T(8,128)(2,1)S(1)} %get-tuple-element.46.refs_0_, bf16[512,128]{1,0:T(8,128)(2,1)S(1)} %collective-permute-done.4.refs_1_, bf16[512,128]{1,0:T(8,128)(2,1)S(1)} %collective-permute-done.5.refs_2_, ...), custom_call_target="tpu_custom_call" | custom-call | flops 268435456 | tf_op jit(solution)/shard_map/pallas_call | solution.py:150
  39.1 1.1 %shard_map.60 = f32[288,128]{1,0:T(8,128)S(1)} custom-call(bf16[512,128]{1,0:T(8,128)(2,1)S(1)} %constant_dynamic-update-slice_fusion.8.refs_0_.refs_4_, bf16[2048,128]{1,0:T(8,128)(2,1)S(1)} %constant_dynamic-update-slice_fusion.25.refs_1_.refs_3_, bf16[2048,128]{1,0:T(8,128)(2,1)S(1)} %collective-permute-done.7.refs_2_.refs_4_), custom_call_target="tpu_custom_call" | custom-call | flops 268435456 | tf_op jit(solution)/shard_map/pallas_call | solution.py:150
  40.2 2.8 %shard_map.61 = (f32[288,128]{1,0:T(8,128)S(1)}, f32[288,128]{1,0:T(8,128)S(1)}, f32[288,128]{1,0:T(8,128)S(1)}) custom-call(bf16[512,128]{1,0:T(8,128)(2,1)S(1)} %collective-permute-done.8.refs_0_, bf16[512,128]{1,0:T(8,128)(2,1)S(1)} %collective-permute-done.9.refs_1_, bf16[512,128]{1,0:T(8,128)(2,1)S(1)} %collective-permute-done.10.refs_2_, ...), custom_call_target="tpu_custom_call" | custom-call | flops 805306368 | tf_op jit(solution)/shard_map/pallas_call | solution.py:150
  43.8 2.9 %collective-permute-start.13 = (f16[288,128]{1,0:T(8,128)(2,1)S(1)}, f16[288,128]{1,0:T(8,128)(2,1)S(1)}, u32[]{:S(2)}, u32[]{:S(2)}) collective-permute-start(f16[288,128]{1,0:T(8,128)(2,1)S(1)} %convert_element_type.74), channel_id=1, source_target_pairs={{0,128},{64,192},{128,0},{192,64},{1,129},{65,193},{129,1},{193,65... | collective-permute-start | bytes 221192 | tf_op jit(solution)/shard_map/ppermute | solution.py:31
  46.7 1.2 %collective-permute-start.14 = (f16[288,128]{1,0:T(8,128)(2,1)S(1)}, f16[288,128]{1,0:T(8,128)(2,1)S(1)}, u32[]{:S(2)}, u32[]{:S(2)}) collective-permute-start(f16[288,128]{1,0:T(8,128)(2,1)S(1)} %convert_element_type.75), channel_id=1, source_target_pairs={{0,192},{64,128},{128,64},{192,0},{1,193},{65,129},{129,65},{193,1... | collective-permute-start | bytes 221192 | tf_op jit(solution)/shard_map/ppermute | solution.py:31
  47.9 2.8 %shard_map.64 = (f32[288,128]{1,0:T(8,128)S(1)}, f32[288,128]{1,0:T(8,128)S(1)}, f32[288,128]{1,0:T(8,128)S(1)}, f32[288,128]{1,0:T(8,128)S(1)}) custom-call(bf16[512,128]{1,0:T(8,128)(2,1)S(1)} %get-tuple-element.46.refs_0_, bf16[512,128]{1,0:T(8,128)(2,1)S(1)} %collective-permute-done.4.refs_1_, bf16[512,128]{1,0:T(8,128)(2,1)S(1)} %collective-permute-done.5.refs_2_, ...), custom_call_target="tpu_custom_call" | custom-call | flops 805306368 | tf_op jit(solution)/shard_map/pallas_call | solution.py:150
  51.4 2.7 %collective-permute-start.18 = (f16[288,128]{1,0:T(8,128)(2,1)S(1)}, f16[288,128]{1,0:T(8,128)(2,1)S(1)}, u32[]{:S(2)}, u32[]{:S(2)}) collective-permute-start(f16[288,128]{1,0:T(8,128)(2,1)S(1)} %convert_element_type.86), channel_id=1, source_target_pairs={{0,8},{4,12},{8,0},{12,4},{1,9},{5,13},{9,1},{13,5},{2,10},{6,14},... | collective-permute-start | bytes 221192 | tf_op jit(solution)/shard_map/ppermute | solution.py:31
  54.2 0.8 %collective-permute-start.17 = (f16[288,128]{1,0:T(8,128)(2,1)S(1)}, f16[288,128]{1,0:T(8,128)(2,1)S(1)}, u32[]{:S(2)}, u32[]{:S(2)}) collective-permute-start(f16[288,128]{1,0:T(8,128)(2,1)S(1)} %convert_element_type.84), channel_id=1, source_target_pairs={{0,4},{4,0},{8,12},{12,8},{1,5},{5,1},{9,13},{13,9},{2,6},{6,2},{1... | collective-permute-start | bytes 221192 | tf_op jit(solution)/shard_map/ppermute | solution.py:31
  55.3 1.0 %collective-permute-start.15 = (f16[144,128]{1,0:T(8,128)(2,1)S(1)}, f16[144,128]{1,0:T(8,128)(2,1)S(1)}, u32[]{:S(2)}, u32[]{:S(2)}) collective-permute-start(f16[144,128]{1,0:T(8,128)(2,1)S(1)} %convert_element_type.80), channel_id=1, source_target_pairs={{0,2},{2,0},{1,3},{3,1},{4,6},{6,4},{5,7},{7,5},{8,10},{10,8},{9,1... | collective-permute-start | bytes 110600 | tf_op jit(solution)/shard_map/ppermute | solution.py:31
  56.3 0.9 %collective-permute-done.18 = f16[288,128]{1,0:T(8,128)(2,1)S(1)} collective-permute-done((f16[288,128]{1,0:T(8,128)(2,1)S(1)}, f16[288,128]{1,0:T(8,128)(2,1)S(1)}, u32[]{:S(2)}, u32[]{:S(2)}) %collective-permute-start.18) | collective-permute-done | bytes 73760 | tf_op jit(solution)/shard_map/ppermute | solution.py:31
  57.3 1.2 %collective-permute-done.17 = f16[288,128]{1,0:T(8,128)(2,1)S(1)} collective-permute-done((f16[288,128]{1,0:T(8,128)(2,1)S(1)}, f16[288,128]{1,0:T(8,128)(2,1)S(1)}, u32[]{:S(2)}, u32[]{:S(2)}) %collective-permute-start.17) | collective-permute-done | bytes 73760 | tf_op jit(solution)/shard_map/ppermute | solution.py:31
  58.5 0.8 %collective-permute-done.15 = f16[144,128]{1,0:T(8,128)(2,1)S(1)} collective-permute-done((f16[144,128]{1,0:T(8,128)(2,1)S(1)}, f16[144,128]{1,0:T(8,128)(2,1)S(1)}, u32[]{:S(2)}, u32[]{:S(2)}) %collective-permute-start.15) | collective-permute-done | bytes 36896 | tf_op jit(solution)/shard_map/ppermute | solution.py:31
  59.7 2.3 %collective-permute-start.22 = (f16[96,128]{1,0:T(8,128)(2,1)S(1)}, f16[96,128]{1,0:T(8,128)(2,1)S(1)}, u32[]{:S(2)}, u32[]{:S(2)}) collective-permute-start(f16[96,128]{1,0:T(8,128)(2,1)S(1)} %convert_element_type.94), channel_id=1, source_target_pairs={{0,48},{16,32},{32,16},{48,0},{1,49},{17,33},{33,17},{49,1},{2,50}... | collective-permute-start | bytes 73736 | tf_op jit(solution)/shard_map/ppermute | solution.py:31
  62.0 2.8 %collective-permute-start.21 = (f16[96,128]{1,0:T(8,128)(2,1)S(1)}, f16[96,128]{1,0:T(8,128)(2,1)S(1)}, u32[]{:S(2)}, u32[]{:S(2)}) collective-permute-start(f16[96,128]{1,0:T(8,128)(2,1)S(1)} %convert_element_type.92), channel_id=1, source_target_pairs={{0,32},{16,48},{32,0},{48,16},{1,33},{17,49},{33,1},{49,17},{2,34}... | collective-permute-start | bytes 73736 | tf_op jit(solution)/shard_map/ppermute | solution.py:31
  64.7 1.5 %collective-permute-start.20 = (f16[96,128]{1,0:T(8,128)(2,1)S(1)}, f16[96,128]{1,0:T(8,128)(2,1)S(1)}, u32[]{:S(2)}, u32[]{:S(2)}) collective-permute-start(f16[96,128]{1,0:T(8,128)(2,1)S(1)} %convert_element_type.90), channel_id=1, source_target_pairs={{0,16},{16,0},{32,48},{48,32},{1,17},{17,1},{33,49},{49,33},{2,18}... | collective-permute-start | bytes 73736 | tf_op jit(solution)/shard_map/ppermute | solution.py:31
  66.3 3.4 %collective-permute-done.21 = f16[96,128]{1,0:T(8,128)(2,1)S(1)} collective-permute-done((f16[96,128]{1,0:T(8,128)(2,1)S(1)}, f16[96,128]{1,0:T(8,128)(2,1)S(1)}, u32[]{:S(2)}, u32[]{:S(2)}) %collective-permute-start.21) | collective-permute-done | bytes 24608 | tf_op jit(solution)/shard_map/ppermute | solution.py:31
  69.7 0.7 shard_map.66
  (78 shorter events, 4.7 us)
Async XLA Ops:
  2.3 10.2 %collective-permute-start = (bf16[192,128]{1,0:T(8,128)(2,1)}, bf16[192,128]{1,0:T(8,128)(2,1)S(1)}, u32[]{:S(2)}, u32[]{:S(2)}) collective-permute-start(bf16[192,128]{1,0:T(8,128)(2,1)} %get-tuple-element.25), channel_id=1, source_target_pairs={{0,16},{16,0},{32,48},{48,32},{1,17},{17,1},{33,49},{49,33},{2,18}... | collective-permute-start | bytes 147464 | tf_op jit(solution)/shard_map/ppermute | solution.py:31
  5.7 8.2 %collective-permute-start.1 = (bf16[192,128]{1,0:T(8,128)(2,1)}, bf16[192,128]{1,0:T(8,128)(2,1)S(1)}, u32[]{:S(2)}, u32[]{:S(2)}) collective-permute-start(bf16[192,128]{1,0:T(8,128)(2,1)} %get-tuple-element.26), channel_id=1, source_target_pairs={{0,32},{16,48},{32,0},{48,16},{1,33},{17,49},{33,1},{49,17},{2,34}... | collective-permute-start | bytes 147464 | tf_op jit(solution)/shard_map/ppermute | solution.py:31
  11.1 6.5 %collective-permute-start.2 = (bf16[192,128]{1,0:T(8,128)(2,1)}, bf16[192,128]{1,0:T(8,128)(2,1)S(1)}, u32[]{:S(2)}, u32[]{:S(2)}) collective-permute-start(bf16[192,128]{1,0:T(8,128)(2,1)} %get-tuple-element.27), channel_id=1, source_target_pairs={{0,48},{16,32},{32,16},{48,0},{1,49},{17,33},{33,17},{49,1},{2,50}... | collective-permute-start | bytes 147464 | tf_op jit(solution)/shard_map/ppermute | solution.py:31
  12.5 5.1 %copy-start = (bf16[192,128]{1,0:T(8,128)(2,1)S(1)}, bf16[192,128]{1,0:T(8,128)(2,1)}, u32[]{:S(2)}) copy-start(bf16[192,128]{1,0:T(8,128)(2,1)} %get-tuple-element.24) | copy-start | bytes 147460
  17.6 12.9 %collective-permute-start.6 = (bf16[512,128]{1,0:T(8,128)(2,1)S(1)}, bf16[512,128]{1,0:T(8,128)(2,1)S(1)}, u32[]{:S(2)}, u32[]{:S(2)}) collective-permute-start(bf16[512,128]{1,0:T(8,128)(2,1)S(1)} %get-tuple-element.46.refs_0_), channel_id=1, source_target_pairs={{0,12},{4,8},{8,4},{12,0},{1,13},{5,9},{9,5},{13,1},{2,14},{6,10},... | collective-permute-start | bytes 393224 | tf_op jit(solution)/shard_map/ppermute | solution.py:31
  18.3 12.2 %collective-permute-start.5 = (bf16[512,128]{1,0:T(8,128)(2,1)S(1)}, bf16[512,128]{1,0:T(8,128)(2,1)S(1)}, u32[]{:S(2)}, u32[]{:S(2)}) collective-permute-start(bf16[512,128]{1,0:T(8,128)(2,1)S(1)} %get-tuple-element.46.refs_0_), channel_id=1, source_target_pairs={{0,8},{4,12},{8,0},{12,4},{1,9},{5,13},{9,1},{13,5},{2,10},{6,14},... | collective-permute-start | bytes 393224 | tf_op jit(solution)/shard_map/ppermute | solution.py:31
  21.0 9.0 %collective-permute-start.4 = (bf16[512,128]{1,0:T(8,128)(2,1)S(1)}, bf16[512,128]{1,0:T(8,128)(2,1)S(1)}, u32[]{:S(2)}, u32[]{:S(2)}) collective-permute-start(bf16[512,128]{1,0:T(8,128)(2,1)S(1)} %get-tuple-element.46.refs_0_), channel_id=1, source_target_pairs={{0,4},{4,0},{8,12},{12,8},{1,5},{5,1},{9,13},{13,9},{2,6},{6,2},{1... | collective-permute-start | bytes 393224 | tf_op jit(solution)/shard_map/ppermute | solution.py:31
  21.9 4.4 %collective-permute-start.3 = (bf16[256,128]{1,0:T(8,128)(2,1)S(1)}, bf16[256,128]{1,0:T(8,128)(2,1)S(1)}, u32[]{:S(2)}, u32[]{:S(2)}) collective-permute-start(bf16[256,128]{1,0:T(8,128)(2,1)S(1)} %get-tuple-element.54), channel_id=1, source_target_pairs={{0,2},{2,0},{1,3},{3,1},{4,6},{6,4},{5,7},{7,5},{8,10},{10,8},{9,1... | collective-permute-start | bytes 196616 | tf_op jit(solution)/shard_map/ppermute | solution.py:31
  26.3 9.6 %collective-permute-start.10 = (bf16[512,128]{1,0:T(8,128)(2,1)S(1)}, bf16[512,128]{1,0:T(8,128)(2,1)S(1)}, u32[]{:S(2)}, u32[]{:S(2)}) collective-permute-start(bf16[512,128]{1,0:T(8,128)(2,1)S(1)} %constant_dynamic-update-slice_fusion.8.refs_0_.refs_4_), channel_id=1, source_target_pairs={{0,192},{64,128},{128,64},{192,0},{1,193},{65,129},{129,65},{193,1... | collective-permute-start | bytes 393224 | tf_op jit(solution)/shard_map/ppermute | solution.py:31
  29.4 6.5 %collective-permute-start.9 = (bf16[512,128]{1,0:T(8,128)(2,1)S(1)}, bf16[512,128]{1,0:T(8,128)(2,1)S(1)}, u32[]{:S(2)}, u32[]{:S(2)}) collective-permute-start(bf16[512,128]{1,0:T(8,128)(2,1)S(1)} %constant_dynamic-update-slice_fusion.8.refs_0_.refs_4_), channel_id=1, source_target_pairs={{0,128},{64,192},{128,0},{192,64},{1,129},{65,193},{129,1},{193,65... | collective-permute-start | bytes 393224 | tf_op jit(solution)/shard_map/ppermute | solution.py:31
  30.0 5.0 %collective-permute-start.8 = (bf16[512,128]{1,0:T(8,128)(2,1)S(1)}, bf16[512,128]{1,0:T(8,128)(2,1)S(1)}, u32[]{:S(2)}, u32[]{:S(2)}) collective-permute-start(bf16[512,128]{1,0:T(8,128)(2,1)S(1)} %constant_dynamic-update-slice_fusion.8.refs_0_.refs_4_), channel_id=1, source_target_pairs={{0,64},{64,0},{128,192},{192,128},{1,65},{65,1},{129,193},{193,129... | collective-permute-start | bytes 393224 | tf_op jit(solution)/shard_map/ppermute | solution.py:31
  30.5 8.5 %collective-permute-start.7 = (bf16[2048,128]{1,0:T(8,128)(2,1)S(1)}, bf16[2048,128]{1,0:T(8,128)(2,1)S(1)}, u32[]{:S(2)}, u32[]{:S(2)}) collective-permute-start(bf16[2048,128]{1,0:T(8,128)(2,1)S(1)} %constant_dynamic-update-slice_fusion.25.refs_1_.refs_3_), channel_id=1, source_target_pairs={{0,1},{1,0},{2,3},{3,2},{4,5},{5,4},{6,7},{7,6},{8,9},{9,8},{10,11... | collective-permute-start | bytes 1572872 | tf_op jit(solution)/shard_map/ppermute | solution.py:31
  35.9 7.2 %collective-permute-start.11 = (bf16[1536,128]{1,0:T(8,128)(2,1)S(1)}, bf16[1536,128]{1,0:T(8,128)(2,1)S(1)}, u32[]{:S(2)}, u32[]{:S(2)}) collective-permute-start(bf16[1536,128]{1,0:T(8,128)(2,1)S(1)} %constant_dynamic-update-slice_fusion.36.refs_4_), channel_id=1, source_target_pairs={{0,1},{1,0},{2,3},{3,2},{4,5},{5,4},{6,7},{7,6},{8,9},{9,8},{10,11... | collective-permute-start | bytes 1179656 | tf_op jit(solution)/shard_map/ppermute | solution.py:31
  36.0 1.9 %collective-permute-start.16 = (bf16[512,128]{1,0:T(8,128)(2,1)S(1)}, bf16[512,128]{1,0:T(8,128)(2,1)S(1)}, u32[]{:S(2)}, u32[]{:S(2)}) collective-permute-start(bf16[512,128]{1,0:T(8,128)(2,1)S(1)} %constant_dynamic-update-slice_fusion.8.refs_0_.refs_4_), channel_id=1, source_target_pairs={{0,1},{1,0},{2,3},{3,2},{4,5},{5,4},{6,7},{7,6},{8,9},{9,8},{10,11... | collective-permute-start | bytes 393224 | tf_op jit(solution)/shard_map/ppermute | solution.py:31
  43.1 11.0 %collective-permute-start.12 = (f16[288,128]{1,0:T(8,128)(2,1)S(1)}, f16[288,128]{1,0:T(8,128)(2,1)S(1)}, u32[]{:S(2)}, u32[]{:S(2)}) collective-permute-start(f16[288,128]{1,0:T(8,128)(2,1)S(1)} %convert_element_type.73), channel_id=1, source_target_pairs={{0,64},{64,0},{128,192},{192,128},{1,65},{65,1},{129,193},{193,129... | collective-permute-start | bytes 221192 | tf_op jit(solution)/shard_map/ppermute | solution.py:31
  43.8 11.3 %collective-permute-start.13 = (f16[288,128]{1,0:T(8,128)(2,1)S(1)}, f16[288,128]{1,0:T(8,128)(2,1)S(1)}, u32[]{:S(2)}, u32[]{:S(2)}) collective-permute-start(f16[288,128]{1,0:T(8,128)(2,1)S(1)} %convert_element_type.74), channel_id=1, source_target_pairs={{0,128},{64,192},{128,0},{192,64},{1,129},{65,193},{129,1},{193,65... | collective-permute-start | bytes 221192 | tf_op jit(solution)/shard_map/ppermute | solution.py:31
  46.7 8.4 %collective-permute-start.14 = (f16[288,128]{1,0:T(8,128)(2,1)S(1)}, f16[288,128]{1,0:T(8,128)(2,1)S(1)}, u32[]{:S(2)}, u32[]{:S(2)}) collective-permute-start(f16[288,128]{1,0:T(8,128)(2,1)S(1)} %convert_element_type.75), channel_id=1, source_target_pairs={{0,192},{64,128},{128,64},{192,0},{1,193},{65,129},{129,65},{193,1... | collective-permute-start | bytes 221192 | tf_op jit(solution)/shard_map/ppermute | solution.py:31
  50.8 5.5 %collective-permute-start.19 = (f16[288,128]{1,0:T(8,128)(2,1)S(1)}, f16[288,128]{1,0:T(8,128)(2,1)S(1)}, u32[]{:S(2)}, u32[]{:S(2)}) collective-permute-start(f16[288,128]{1,0:T(8,128)(2,1)S(1)} %convert_element_type.88), channel_id=1, source_target_pairs={{0,12},{4,8},{8,4},{12,0},{1,13},{5,9},{9,5},{13,1},{2,14},{6,10},... | collective-permute-start | bytes 221192 | tf_op jit(solution)/shard_map/ppermute | solution.py:31
  51.4 5.9 %collective-permute-start.18 = (f16[288,128]{1,0:T(8,128)(2,1)S(1)}, f16[288,128]{1,0:T(8,128)(2,1)S(1)}, u32[]{:S(2)}, u32[]{:S(2)}) collective-permute-start(f16[288,128]{1,0:T(8,128)(2,1)S(1)} %convert_element_type.86), channel_id=1, source_target_pairs={{0,8},{4,12},{8,0},{12,4},{1,9},{5,13},{9,1},{13,5},{2,10},{6,14},... | collective-permute-start | bytes 221192 | tf_op jit(solution)/shard_map/ppermute | solution.py:31
  54.2 4.4 %collective-permute-start.17 = (f16[288,128]{1,0:T(8,128)(2,1)S(1)}, f16[288,128]{1,0:T(8,128)(2,1)S(1)}, u32[]{:S(2)}, u32[]{:S(2)}) collective-permute-start(f16[288,128]{1,0:T(8,128)(2,1)S(1)} %convert_element_type.84), channel_id=1, source_target_pairs={{0,4},{4,0},{8,12},{12,8},{1,5},{5,1},{9,13},{13,9},{2,6},{6,2},{1... | collective-permute-start | bytes 221192 | tf_op jit(solution)/shard_map/ppermute | solution.py:31
  55.3 4.0 %collective-permute-start.15 = (f16[144,128]{1,0:T(8,128)(2,1)S(1)}, f16[144,128]{1,0:T(8,128)(2,1)S(1)}, u32[]{:S(2)}, u32[]{:S(2)}) collective-permute-start(f16[144,128]{1,0:T(8,128)(2,1)S(1)} %convert_element_type.80), channel_id=1, source_target_pairs={{0,2},{2,0},{1,3},{3,1},{4,6},{6,4},{5,7},{7,5},{8,10},{10,8},{9,1... | collective-permute-start | bytes 110600 | tf_op jit(solution)/shard_map/ppermute | solution.py:31
  59.7 6.6 %collective-permute-start.22 = (f16[96,128]{1,0:T(8,128)(2,1)S(1)}, f16[96,128]{1,0:T(8,128)(2,1)S(1)}, u32[]{:S(2)}, u32[]{:S(2)}) collective-permute-start(f16[96,128]{1,0:T(8,128)(2,1)S(1)} %convert_element_type.94), channel_id=1, source_target_pairs={{0,48},{16,32},{32,16},{48,0},{1,49},{17,33},{33,17},{49,1},{2,50}... | collective-permute-start | bytes 73736 | tf_op jit(solution)/shard_map/ppermute | solution.py:31
  62.0 7.7 %collective-permute-start.21 = (f16[96,128]{1,0:T(8,128)(2,1)S(1)}, f16[96,128]{1,0:T(8,128)(2,1)S(1)}, u32[]{:S(2)}, u32[]{:S(2)}) collective-permute-start(f16[96,128]{1,0:T(8,128)(2,1)S(1)} %convert_element_type.92), channel_id=1, source_target_pairs={{0,32},{16,48},{32,0},{48,16},{1,33},{17,49},{33,1},{49,17},{2,34}... | collective-permute-start | bytes 73736 | tf_op jit(solution)/shard_map/ppermute | solution.py:31
  64.7 5.0 %collective-permute-start.20 = (f16[96,128]{1,0:T(8,128)(2,1)S(1)}, f16[96,128]{1,0:T(8,128)(2,1)S(1)}, u32[]{:S(2)}, u32[]{:S(2)}) collective-permute-start(f16[96,128]{1,0:T(8,128)(2,1)S(1)} %convert_element_type.90), channel_id=1, source_target_pairs={{0,16},{16,0},{32,48},{48,32},{1,17},{17,1},{33,49},{49,33},{2,18}... | collective-permute-start | bytes 73736 | tf_op jit(solution)/shard_map/ppermute | solution.py:31
where the time goes:
time: 70.7 us; the launch traced here: 70.4 us
  starting transfers between devices  35.4 us (50%)
  waiting for transfers between devices  21.2 us (30%)
  Pallas kernels  10.8 us (15%)
  local copies, waits for them, and re-layouts  1.72 us (2%)
  between operations  0.98 us (1%)
    ppermute x23, starting transfers between devices, swap(): return lax.ppermute(value, axes, [(i, i ^ k) for i in range(size)])  35.4 us
    ppermute x23, waiting for transfers between devices, swap(): return lax.ppermute(value, axes, [(i, i ^ k) for i in range(size)])  21.2 us
    pallas_call x4, Pallas kernels, attention(): pl.pallas_call(functools.partial(attend_kernel, rows, span, n_q, n_kv, le...  7.93 us
    pallas_call x1, Pallas kernels, both_ways(): pl.pallas_call(split_heads, out_shape=[message] * heads, in_specs=[SMEM]...  1.69 us
    unnamed x28, local copies, waits for them, and re-layouts  1.65 us
  transfers between devices with their start and end apart: 23, of which 10 were waited for; matrix products, arithmetic and copies ran while one was open for 3% of the time, Pallas kernels for 11%

commit v1 on v0

--- a/solution.py
+++ b/solution.py
@@ -90,23 +90,28 @@
     keys = [(ref, at) for ref in kv_refs for at in range(0, ref.shape[0], 2 * span)]
     blocks = [(i, j) for i, ref in enumerate(q_refs) for j in range(ref.shape[0] // (2 * rows))]
     step = GROUP // rows
-    for g in range(0, len(blocks), step):
-        group = blocks[g : g + step]
-        size = rows * len(group)
-        queries = joined([q_refs[i][2 * rows * j : 2 * rows * j + rows, :] for i, j in group])
-        top = None
-        for n, (ref, at) in enumerate(keys):
-            logits = lax.dot_general(
-                queries, ref[at : at + span, :], (((1,), (1,)), ((), ())), preferred_element_type=jnp.float32
-            )
-            scores[:size, n * span : (n + 1) * span] = logits
-            for c in range(0, span, LANES):
-                part = logits[:, c : c + LANES]
-                top = part if top is None else jnp.maximum(top, part)
-        peak = jnp.max(top, axis=1, keepdims=True) * SCALE
+    groups = [blocks[g : g + step] for g in range(0, len(blocks), step)]
+    tops = [None] * len(groups)
+
+    def score(g, n):
+        queries = joined([q_refs[i][2 * rows * j : 2 * rows * j + rows, :] for i, j in groups[g]])
+        ref, at = keys[n]
+        logits = lax.dot_general(
+            queries, ref[at : at + span, :], (((1,), (1,)), ((), ())), preferred_element_type=jnp.float32
+        )
+        scores[g % 2, : queries.shape[0], n * span : (n + 1) * span] = logits
+        for c in range(0, span, LANES):
+            part = logits[:, c : c + LANES]
+            tops[g] = part if tops[g] is None else jnp.maximum(tops[g], part)
+
+    for n in range(len(keys)):
+        score(0, n)
+    for at_group, group in enumerate(groups):
+        g, size = at_group * step, rows * len(group)
+        peak = jnp.max(tops[at_group], axis=1, keepdims=True) * SCALE
         total, number = None, None
         for n, (ref, at) in enumerate(keys):
-            weights = jnp.exp2(scores[:size, n * span : (n + 1) * span] * SCALE - peak)
+            weights = jnp.exp2(scores[at_group % 2, :size, n * span : (n + 1) * span] * SCALE - peak)
             for c in range(0, span, LANES):
                 part = weights[:, c : c + LANES]
                 total = part if total is None else total + part
@@ -114,6 +119,8 @@
                 weights.astype(jnp.bfloat16), ref[at + span : at + 2 * span, :], preferred_element_type=jnp.float32
             )
             number = part if number is None else number + part
+            if at_group + 1 < len(groups):
+                score(at_group + 1, n)
         total = jnp.sum(total, axis=1, keepdims=True)
         mean = number / total
         level = jnp.broadcast_to(peak + jnp.log2(total), (size, LANES))
@@ -152,7 +159,7 @@
         out_shape=[jax.ShapeDtypeStruct(s, jnp.float32) for s in shapes],
         in_specs=[VMEM] * (n_q + n_kv + len(before)),
         out_specs=[VMEM] * len(shapes),
-        scratch_shapes=[pltpu.VMEM((GROUP, keys), jnp.float32)],
+        scratch_shapes=[pltpu.VMEM((2, GROUP, keys), jnp.float32)],
         compiler_params=PARAMS,
         cost_estimate=pl.CostEstimate(flops=4 * whole * keys * HEAD, bytes_accessed=0, transcendentals=whole * keys),
     )(*q_blocks, *kv_stacks, *before)
@@ -216,8 +223,8 @@
         in_specs=[SMEM] + [HBM] * 4,
         out_specs=[VMEM] * heads,
         scratch_shapes=[pltpu.SemaphoreType.DMA((4 * heads,))],
-        compiler_params=WIDE,
-    )(place, rep_a, val_a, rep_b, val_b)
+        compiler_params=SMALL,
+    )(place, *(pltpu.with_memory_space_constraint(x, pltpu.HBM) for x in (rep_a, val_a, rep_b, val_b)))
     took = exchange(sent, HEAD_AXIS)
     edges = (0, rows_a, 2 * rows_a, 2 * rows_a + rows_b, 2 * (rows_a + rows_b))
     own_a = jnp.concatenate([t[edges[i] : edges[i + 1]] for i in (0, 1) for t in took])

time: 70.7 us -> 69.3 us (0.980)
  local copies, waits for them, and re-layouts: 1.72 us -> 0.31 us
  waiting for transfers between devices: 21.2 us -> 22.4 us
  Pallas kernels: 10.8 us -> 9.73 us
    unnamed x28 -> x26, local copies, waits for them, and re-layouts: 1.65 us -> 0.23 us
    ppermute x23, waiting for transfers between devices: 21.2 us -> 22.4 us  [swap(): return lax.ppermute(value, axes, [(i, i ^ k) for i in range(size)])]
  transfers between devices with their start and end apart: 23 -> 23, of which waited for: 10 -> 10; matrix products, arithmetic and copies ran while one was open for 3% -> 1% of each run, Pallas kernels for 11% -> 11%
where the time goes in v1:
time: 69.3 us; the launch traced here: 69.1 us
  starting transfers between devices  35.4 us (51%)
  waiting for transfers between devices  22.4 us (32%)
  Pallas kernels  9.73 us (14%)
  between operations  0.99 us (1%)
    ppermute x23, starting transfers between devices, swap(): return lax.ppermute(value, axes, [(i, i ^ k) for i in range(size)])  35.4 us
    ppermute x23, waiting for transfers between devices, swap(): return lax.ppermute(value, axes, [(i, i ^ k) for i in range(size)])  22.4 us
    pallas_call x4, Pallas kernels, attention(): pl.pallas_call(functools.partial(attend_kernel, rows, span, n_q, n_kv, le...  7.5 us
  transfers between devices with their start and end apart: 23, of which 10 were waited for; matrix products, arithmetic and copies ran while one was open for 1% of the time, Pallas kernels for 11%

profile of v1, /device:TPU:4, one launch (start us, length us, event | category | flops | bytes accessed | tf_op | source)
XLA Modules:
  0.0 69.1 jit_solution(403799506428189114)
XLA Ops:
  0.6 1.0 %shard_map.59 = (bf16[192,128]{1,0:T(8,128)(2,1)S(1)}, bf16[192,128]{1,0:T(8,128)(2,1)S(1)}, bf16[192,128]{1,0:T(8,128)(2,1)S(1)}, bf16[192,128]{1,0:T(8,128)(2,1)S(1)}) custom-call(s32[1]{0:T(128)} %bitcast.place, bf16[32,512]{1,0:T(8,128)(2,1)} %refs_0_.1, bf16[32,512]{1,0:T(8,128)(2,1)} %refs_1_.1, bf16[64,512]{1,0:T(8,128)(2,1)} %refs_2_.1, ...), custom_call_target="tpu_custom_call" | custom-call | tf_op jit(solution)/shard_map/pallas_call | solution.py:220
  1.7 3.4 %collective-permute-start = (bf16[192,128]{1,0:T(8,128)(2,1)S(1)}, bf16[192,128]{1,0:T(8,128)(2,1)S(1)}, u32[]{:S(2)}, u32[]{:S(2)}) collective-permute-start(bf16[192,128]{1,0:T(8,128)(2,1)S(1)} %get-tuple-element.25), channel_id=1, source_target_pairs={{0,16},{16,0},{32,48},{48,32},{1,17},{17,1},{33,49},{49,33},{2,18}... | collective-permute-start | bytes 147464 | tf_op jit(solution)/shard_map/ppermute | solution.py:31
  5.0 5.4 %collective-permute-start.1 = (bf16[192,128]{1,0:T(8,128)(2,1)S(1)}, bf16[192,128]{1,0:T(8,128)(2,1)S(1)}, u32[]{:S(2)}, u32[]{:S(2)}) collective-permute-start(bf16[192,128]{1,0:T(8,128)(2,1)S(1)} %get-tuple-element.26), channel_id=1, source_target_pairs={{0,32},{16,48},{32,0},{48,16},{1,33},{17,49},{33,1},{49,17},{2,34}... | collective-permute-start | bytes 147464 | tf_op jit(solution)/shard_map/ppermute | solution.py:31
  10.5 2.6 %collective-permute-done.1 = bf16[192,128]{1,0:T(8,128)(2,1)S(1)} collective-permute-done((bf16[192,128]{1,0:T(8,128)(2,1)S(1)}, bf16[192,128]{1,0:T(8,128)(2,1)S(1)}, u32[]{:S(2)}, u32[]{:S(2)}) %collective-permute-start.1) | collective-permute-done | bytes 49184 | tf_op jit(solution)/shard_map/ppermute | solution.py:31
  13.0 3.7 %collective-permute-done.2 = bf16[192,128]{1,0:T(8,128)(2,1)S(1)} collective-permute-done((bf16[192,128]{1,0:T(8,128)(2,1)S(1)}, bf16[192,128]{1,0:T(8,128)(2,1)S(1)}, u32[]{:S(2)}, u32[]{:S(2)}) %collective-permute-start.2) | collective-permute-done | bytes 49184 | tf_op jit(solution)/shard_map/ppermute | solution.py:31
  17.4 2.7 %collective-permute-start.5 = (bf16[512,128]{1,0:T(8,128)(2,1)S(1)}, bf16[512,128]{1,0:T(8,128)(2,1)S(1)}, u32[]{:S(2)}, u32[]{:S(2)}) collective-permute-start(bf16[512,128]{1,0:T(8,128)(2,1)S(1)} %get-tuple-element.46.refs_0_), channel_id=1, source_target_pairs={{0,8},{4,12},{8,0},{12,4},{1,9},{5,13},{9,1},{13,5},{2,10},{6,14},... | collective-permute-start | bytes 393224 | tf_op jit(solution)/shard_map/ppermute | solution.py:31
  20.1 0.8 %collective-permute-start.4 = (bf16[512,128]{1,0:T(8,128)(2,1)S(1)}, bf16[512,128]{1,0:T(8,128)(2,1)S(1)}, u32[]{:S(2)}, u32[]{:S(2)}) collective-permute-start(bf16[512,128]{1,0:T(8,128)(2,1)S(1)} %get-tuple-element.46.refs_0_), channel_id=1, source_target_pairs={{0,4},{4,0},{8,12},{12,8},{1,5},{5,1},{9,13},{13,9},{2,6},{6,2},{1... | collective-permute-start | bytes 393224 | tf_op jit(solution)/shard_map/ppermute | solution.py:31
  21.0 1.0 %collective-permute-start.3 = (bf16[256,128]{1,0:T(8,128)(2,1)S(1)}, bf16[256,128]{1,0:T(8,128)(2,1)S(1)}, u32[]{:S(2)}, u32[]{:S(2)}) collective-permute-start(bf16[256,128]{1,0:T(8,128)(2,1)S(1)} %get-tuple-element.54), channel_id=1, source_target_pairs={{0,2},{2,0},{1,3},{3,1},{4,6},{6,4},{5,7},{7,5},{8,10},{10,8},{9,1... | collective-permute-start | bytes 196616 | tf_op jit(solution)/shard_map/ppermute | solution.py:31
  22.1 3.2 %collective-permute-done.3 = bf16[256,128]{1,0:T(8,128)(2,1)S(1)} collective-permute-done((bf16[256,128]{1,0:T(8,128)(2,1)S(1)}, bf16[256,128]{1,0:T(8,128)(2,1)S(1)}, u32[]{:S(2)}, u32[]{:S(2)}) %collective-permute-start.3) | collective-permute-done | bytes 65568 | tf_op jit(solution)/shard_map/ppermute | solution.py:31
  25.4 3.1 %collective-permute-start.10 = (bf16[512,128]{1,0:T(8,128)(2,1)S(1)}, bf16[512,128]{1,0:T(8,128)(2,1)S(1)}, u32[]{:S(2)}, u32[]{:S(2)}) collective-permute-start(bf16[512,128]{1,0:T(8,128)(2,1)S(1)} %constant_dynamic-update-slice_fusion.8.refs_0_.refs_4_), channel_id=1, source_target_pairs={{0,192},{64,128},{128,64},{192,0},{1,193},{65,129},{129,65},{193,1... | collective-permute-start | bytes 393224 | tf_op jit(solution)/shard_map/ppermute | solution.py:31
  28.5 0.6 collective-permute-start.9
  29.8 4.3 %collective-permute-done.8.refs_0_ = bf16[512,128]{1,0:T(8,128)(2,1)S(1)} collective-permute-done((bf16[512,128]{1,0:T(8,128)(2,1)S(1)}, bf16[512,128]{1,0:T(8,128)(2,1)S(1)}, u32[]{:S(2)}, u32[]{:S(2)}) %collective-permute-start.8) | collective-permute-done | bytes 131104 | tf_op jit(solution)/shard_map/ppermute | solution.py:31
  34.1 0.9 %collective-permute-done.9.refs_1_ = bf16[512,128]{1,0:T(8,128)(2,1)S(1)} collective-permute-done((bf16[512,128]{1,0:T(8,128)(2,1)S(1)}, bf16[512,128]{1,0:T(8,128)(2,1)S(1)}, u32[]{:S(2)}, u32[]{:S(2)}) %collective-permute-start.9) | collective-permute-done | bytes 131104 | tf_op jit(solution)/shard_map/ppermute | solution.py:31
  35.6 1.4 %collective-permute-done.16.refs_5_ = bf16[512,128]{1,0:T(8,128)(2,1)S(1)} collective-permute-done((bf16[512,128]{1,0:T(8,128)(2,1)S(1)}, bf16[512,128]{1,0:T(8,128)(2,1)S(1)}, u32[]{:S(2)}, u32[]{:S(2)}) %collective-permute-start.16) | collective-permute-done | bytes 131104 | tf_op jit(solution)/shard_map/ppermute | solution.py:31
  37.0 1.1 %shard_map.63 = (f32[1024,128]{1,0:T(8,128)S(1)}, f32[1024,128]{1,0:T(8,128)S(1)}) custom-call(bf16[512,128]{1,0:T(8,128)(2,1)S(1)} %get-tuple-element.46.refs_0_, bf16[512,128]{1,0:T(8,128)(2,1)S(1)} %collective-permute-done.4.refs_1_, bf16[512,128]{1,0:T(8,128)(2,1)S(1)} %collective-permute-done.5.refs_2_, ...), custom_call_target="tpu_custom_call" | custom-call | flops 268435456 | tf_op jit(solution)/shard_map/pallas_call | solution.py:157
  38.1 1.1 %shard_map.60 = f32[288,128]{1,0:T(8,128)S(1)} custom-call(bf16[512,128]{1,0:T(8,128)(2,1)S(1)} %constant_dynamic-update-slice_fusion.8.refs_0_.refs_4_, bf16[2048,128]{1,0:T(8,128)(2,1)S(1)} %constant_dynamic-update-slice_fusion.25.refs_1_.refs_3_, bf16[2048,128]{1,0:T(8,128)(2,1)S(1)} %collective-permute-done.7.refs_2_.refs_4_), custom_call_target="tpu_custom_call" | custom-call | flops 268435456 | tf_op jit(solution)/shard_map/pallas_call | solution.py:157
  39.2 2.7 %shard_map.61 = (f32[288,128]{1,0:T(8,128)S(1)}, f32[288,128]{1,0:T(8,128)S(1)}, f32[288,128]{1,0:T(8,128)S(1)}) custom-call(bf16[512,128]{1,0:T(8,128)(2,1)S(1)} %collective-permute-done.8.refs_0_, bf16[512,128]{1,0:T(8,128)(2,1)S(1)} %collective-permute-done.9.refs_1_, bf16[512,128]{1,0:T(8,128)(2,1)S(1)} %collective-permute-done.10.refs_2_, ...), custom_call_target="tpu_custom_call" | custom-call | flops 805306368 | tf_op jit(solution)/shard_map/pallas_call | solution.py:157
  42.0 0.6 collective-permute-start.12
  42.7 2.9 %collective-permute-start.13 = (f16[288,128]{1,0:T(8,128)(2,1)S(1)}, f16[288,128]{1,0:T(8,128)(2,1)S(1)}, u32[]{:S(2)}, u32[]{:S(2)}) collective-permute-start(f16[288,128]{1,0:T(8,128)(2,1)S(1)} %convert_element_type.74), channel_id=1, source_target_pairs={{0,128},{64,192},{128,0},{192,64},{1,129},{65,193},{129,1},{193,65... | collective-permute-start | bytes 221192 | tf_op jit(solution)/shard_map/ppermute | solution.py:31
  45.6 1.2 %collective-permute-start.14 = (f16[288,128]{1,0:T(8,128)(2,1)S(1)}, f16[288,128]{1,0:T(8,128)(2,1)S(1)}, u32[]{:S(2)}, u32[]{:S(2)}) collective-permute-start(f16[288,128]{1,0:T(8,128)(2,1)S(1)} %convert_element_type.75), channel_id=1, source_target_pairs={{0,192},{64,128},{128,64},{192,0},{1,193},{65,129},{129,65},{193,1... | collective-permute-start | bytes 221192 | tf_op jit(solution)/shard_map/ppermute | solution.py:31
  46.8 2.6 %shard_map.64 = (f32[288,128]{1,0:T(8,128)S(1)}, f32[288,128]{1,0:T(8,128)S(1)}, f32[288,128]{1,0:T(8,128)S(1)}, f32[288,128]{1,0:T(8,128)S(1)}) custom-call(bf16[512,128]{1,0:T(8,128)(2,1)S(1)} %get-tuple-element.46.refs_0_, bf16[512,128]{1,0:T(8,128)(2,1)S(1)} %collective-permute-done.4.refs_1_, bf16[512,128]{1,0:T(8,128)(2,1)S(1)} %collective-permute-done.5.refs_2_, ...), custom_call_target="tpu_custom_call" | custom-call | flops 805306368 | tf_op jit(solution)/shard_map/pallas_call | solution.py:157
  50.1 2.7 %collective-permute-start.18 = (f16[288,128]{1,0:T(8,128)(2,1)S(1)}, f16[288,128]{1,0:T(8,128)(2,1)S(1)}, u32[]{:S(2)}, u32[]{:S(2)}) collective-permute-start(f16[288,128]{1,0:T(8,128)(2,1)S(1)} %convert_element_type.86), channel_id=1, source_target_pairs={{0,8},{4,12},{8,0},{12,4},{1,9},{5,13},{9,1},{13,5},{2,10},{6,14},... | collective-permute-start | bytes 221192 | tf_op jit(solution)/shard_map/ppermute | solution.py:31
  52.9 0.8 %collective-permute-start.17 = (f16[288,128]{1,0:T(8,128)(2,1)S(1)}, f16[288,128]{1,0:T(8,128)(2,1)S(1)}, u32[]{:S(2)}, u32[]{:S(2)}) collective-permute-start(f16[288,128]{1,0:T(8,128)(2,1)S(1)} %convert_element_type.84), channel_id=1, source_target_pairs={{0,4},{4,0},{8,12},{12,8},{1,5},{5,1},{9,13},{13,9},{2,6},{6,2},{1... | collective-permute-start | bytes 221192 | tf_op jit(solution)/shard_map/ppermute | solution.py:31
  54.0 1.0 %collective-permute-start.15 = (f16[144,128]{1,0:T(8,128)(2,1)S(1)}, f16[144,128]{1,0:T(8,128)(2,1)S(1)}, u32[]{:S(2)}, u32[]{:S(2)}) collective-permute-start(f16[144,128]{1,0:T(8,128)(2,1)S(1)} %convert_element_type.80), channel_id=1, source_target_pairs={{0,2},{2,0},{1,3},{3,1},{4,6},{6,4},{5,7},{7,5},{8,10},{10,8},{9,1... | collective-permute-start | bytes 110600 | tf_op jit(solution)/shard_map/ppermute | solution.py:31
  55.0 1.0 %collective-permute-done.18 = f16[288,128]{1,0:T(8,128)(2,1)S(1)} collective-permute-done((f16[288,128]{1,0:T(8,128)(2,1)S(1)}, f16[288,128]{1,0:T(8,128)(2,1)S(1)}, u32[]{:S(2)}, u32[]{:S(2)}) %collective-permute-start.18) | collective-permute-done | bytes 73760 | tf_op jit(solution)/shard_map/ppermute | solution.py:31
  56.0 1.2 %collective-permute-done.17 = f16[288,128]{1,0:T(8,128)(2,1)S(1)} collective-permute-done((f16[288,128]{1,0:T(8,128)(2,1)S(1)}, f16[288,128]{1,0:T(8,128)(2,1)S(1)}, u32[]{:S(2)}, u32[]{:S(2)}) %collective-permute-start.17) | collective-permute-done | bytes 73760 | tf_op jit(solution)/shard_map/ppermute | solution.py:31
  57.2 0.8 %collective-permute-done.15 = f16[144,128]{1,0:T(8,128)(2,1)S(1)} collective-permute-done((f16[144,128]{1,0:T(8,128)(2,1)S(1)}, f16[144,128]{1,0:T(8,128)(2,1)S(1)}, u32[]{:S(2)}, u32[]{:S(2)}) %collective-permute-start.15) | collective-permute-done | bytes 36896 | tf_op jit(solution)/shard_map/ppermute | solution.py:31
  58.4 2.3 %collective-permute-start.22 = (f16[96,128]{1,0:T(8,128)(2,1)S(1)}, f16[96,128]{1,0:T(8,128)(2,1)S(1)}, u32[]{:S(2)}, u32[]{:S(2)}) collective-permute-start(f16[96,128]{1,0:T(8,128)(2,1)S(1)} %convert_element_type.94), channel_id=1, source_target_pairs={{0,48},{16,32},{32,16},{48,0},{1,49},{17,33},{33,17},{49,1},{2,50}... | collective-permute-start | bytes 73736 | tf_op jit(solution)/shard_map/ppermute | solution.py:31
  60.7 2.8 %collective-permute-start.21 = (f16[96,128]{1,0:T(8,128)(2,1)S(1)}, f16[96,128]{1,0:T(8,128)(2,1)S(1)}, u32[]{:S(2)}, u32[]{:S(2)}) collective-permute-start(f16[96,128]{1,0:T(8,128)(2,1)S(1)} %convert_element_type.92), channel_id=1, source_target_pairs={{0,32},{16,48},{32,0},{48,16},{1,33},{17,49},{33,1},{49,17},{2,34}... | collective-permute-start | bytes 73736 | tf_op jit(solution)/shard_map/ppermute | solution.py:31
  63.4 1.5 %collective-permute-start.20 = (f16[96,128]{1,0:T(8,128)(2,1)S(1)}, f16[96,128]{1,0:T(8,128)(2,1)S(1)}, u32[]{:S(2)}, u32[]{:S(2)}) collective-permute-start(f16[96,128]{1,0:T(8,128)(2,1)S(1)} %convert_element_type.90), channel_id=1, source_target_pairs={{0,16},{16,0},{32,48},{48,32},{1,17},{17,1},{33,49},{49,33},{2,18}... | collective-permute-start | bytes 73736 | tf_op jit(solution)/shard_map/ppermute | solution.py:31
  65.0 3.4 %collective-permute-done.21 = f16[96,128]{1,0:T(8,128)(2,1)S(1)} collective-permute-done((f16[96,128]{1,0:T(8,128)(2,1)S(1)}, f16[96,128]{1,0:T(8,128)(2,1)S(1)}, u32[]{:S(2)}, u32[]{:S(2)}) %collective-permute-start.21) | collective-permute-done | bytes 24608 | tf_op jit(solution)/shard_map/ppermute | solution.py:31
  68.4 0.7 %shard_map.66 = (f32[32,512]{1,0:T(8,128)}, f32[64,512]{1,0:T(8,128)}) custom-call(s32[1]{0:T(128)} %bitcast.place, f32[96,128]{1,0:T(8,128)S(1)} %get-tuple-element.42.refs_0_, f32[96,128]{1,0:T(8,128)S(1)} %convert_element_type.91.refs_1_, f32[96,128]{1,0:T(8,128)S(1)} %convert_element_type.93.refs_2_, f32[96,128]{1,0:T(8,128)S(1)} %convert_element_type.95.refs_3_), custom_call_target="tpu_custom_call" | custom-call | tf_op jit(solution)/shard_map/pallas_call | solution.py:275
  (76 shorter events, 3.5 us)
Async XLA Ops:
  1.7 8.8 %collective-permute-start = (bf16[192,128]{1,0:T(8,128)(2,1)S(1)}, bf16[192,128]{1,0:T(8,128)(2,1)S(1)}, u32[]{:S(2)}, u32[]{:S(2)}) collective-permute-start(bf16[192,128]{1,0:T(8,128)(2,1)S(1)} %get-tuple-element.25), channel_id=1, source_target_pairs={{0,16},{16,0},{32,48},{48,32},{1,17},{17,1},{33,49},{49,33},{2,18}... | collective-permute-start | bytes 147464 | tf_op jit(solution)/shard_map/ppermute | solution.py:31
  5.0 8.0 %collective-permute-start.1 = (bf16[192,128]{1,0:T(8,128)(2,1)S(1)}, bf16[192,128]{1,0:T(8,128)(2,1)S(1)}, u32[]{:S(2)}, u32[]{:S(2)}) collective-permute-start(bf16[192,128]{1,0:T(8,128)(2,1)S(1)} %get-tuple-element.26), channel_id=1, source_target_pairs={{0,32},{16,48},{32,0},{48,16},{1,33},{17,49},{33,1},{49,17},{2,34}... | collective-permute-start | bytes 147464 | tf_op jit(solution)/shard_map/ppermute | solution.py:31
  10.4 6.3 %collective-permute-start.2 = (bf16[192,128]{1,0:T(8,128)(2,1)S(1)}, bf16[192,128]{1,0:T(8,128)(2,1)S(1)}, u32[]{:S(2)}, u32[]{:S(2)}) collective-permute-start(bf16[192,128]{1,0:T(8,128)(2,1)S(1)} %get-tuple-element.27), channel_id=1, source_target_pairs={{0,48},{16,32},{32,16},{48,0},{1,49},{17,33},{33,17},{49,1},{2,50}... | collective-permute-start | bytes 147464 | tf_op jit(solution)/shard_map/ppermute | solution.py:31
  16.8 12.9 %collective-permute-start.6 = (bf16[512,128]{1,0:T(8,128)(2,1)S(1)}, bf16[512,128]{1,0:T(8,128)(2,1)S(1)}, u32[]{:S(2)}, u32[]{:S(2)}) collective-permute-start(bf16[512,128]{1,0:T(8,128)(2,1)S(1)} %get-tuple-element.46.refs_0_), channel_id=1, source_target_pairs={{0,12},{4,8},{8,4},{12,0},{1,13},{5,9},{9,5},{13,1},{2,14},{6,10},... | collective-permute-start | bytes 393224 | tf_op jit(solution)/shard_map/ppermute | solution.py:31
  17.4 12.2 %collective-permute-start.5 = (bf16[512,128]{1,0:T(8,128)(2,1)S(1)}, bf16[512,128]{1,0:T(8,128)(2,1)S(1)}, u32[]{:S(2)}, u32[]{:S(2)}) collective-permute-start(bf16[512,128]{1,0:T(8,128)(2,1)S(1)} %get-tuple-element.46.refs_0_), channel_id=1, source_target_pairs={{0,8},{4,12},{8,0},{12,4},{1,9},{5,13},{9,1},{13,5},{2,10},{6,14},... | collective-permute-start | bytes 393224 | tf_op jit(solution)/shard_map/ppermute | solution.py:31
  20.1 9.0 %collective-permute-start.4 = (bf16[512,128]{1,0:T(8,128)(2,1)S(1)}, bf16[512,128]{1,0:T(8,128)(2,1)S(1)}, u32[]{:S(2)}, u32[]{:S(2)}) collective-permute-start(bf16[512,128]{1,0:T(8,128)(2,1)S(1)} %get-tuple-element.46.refs_0_), channel_id=1, source_target_pairs={{0,4},{4,0},{8,12},{12,8},{1,5},{5,1},{9,13},{13,9},{2,6},{6,2},{1... | collective-permute-start | bytes 393224 | tf_op jit(solution)/shard_map/ppermute | solution.py:31
  21.0 4.4 %collective-permute-start.3 = (bf16[256,128]{1,0:T(8,128)(2,1)S(1)}, bf16[256,128]{1,0:T(8,128)(2,1)S(1)}, u32[]{:S(2)}, u32[]{:S(2)}) collective-permute-start(bf16[256,128]{1,0:T(8,128)(2,1)S(1)} %get-tuple-element.54), channel_id=1, source_target_pairs={{0,2},{2,0},{1,3},{3,1},{4,6},{6,4},{5,7},{7,5},{8,10},{10,8},{9,1... | collective-permute-start | bytes 196616 | tf_op jit(solution)/shard_map/ppermute | solution.py:31
  25.4 9.6 %collective-permute-start.10 = (bf16[512,128]{1,0:T(8,128)(2,1)S(1)}, bf16[512,128]{1,0:T(8,128)(2,1)S(1)}, u32[]{:S(2)}, u32[]{:S(2)}) collective-permute-start(bf16[512,128]{1,0:T(8,128)(2,1)S(1)} %constant_dynamic-update-slice_fusion.8.refs_0_.refs_4_), channel_id=1, source_target_pairs={{0,192},{64,128},{128,64},{192,0},{1,193},{65,129},{129,65},{193,1... | collective-permute-start | bytes 393224 | tf_op jit(solution)/shard_map/ppermute | solution.py:31
  28.5 6.5 %collective-permute-start.9 = (bf16[512,128]{1,0:T(8,128)(2,1)S(1)}, bf16[512,128]{1,0:T(8,128)(2,1)S(1)}, u32[]{:S(2)}, u32[]{:S(2)}) collective-permute-start(bf16[512,128]{1,0:T(8,128)(2,1)S(1)} %constant_dynamic-update-slice_fusion.8.refs_0_.refs_4_), channel_id=1, source_target_pairs={{0,128},{64,192},{128,0},{192,64},{1,129},{65,193},{129,1},{193,65... | collective-permute-start | bytes 393224 | tf_op jit(solution)/shard_map/ppermute | solution.py:31
  29.1 5.0 %collective-permute-start.8 = (bf16[512,128]{1,0:T(8,128)(2,1)S(1)}, bf16[512,128]{1,0:T(8,128)(2,1)S(1)}, u32[]{:S(2)}, u32[]{:S(2)}) collective-permute-start(bf16[512,128]{1,0:T(8,128)(2,1)S(1)} %constant_dynamic-update-slice_fusion.8.refs_0_.refs_4_), channel_id=1, source_target_pairs={{0,64},{64,0},{128,192},{192,128},{1,65},{65,1},{129,193},{193,129... | collective-permute-start | bytes 393224 | tf_op jit(solution)/shard_map/ppermute | solution.py:31
  29.7 8.4 %collective-permute-start.7 = (bf16[2048,128]{1,0:T(8,128)(2,1)S(1)}, bf16[2048,128]{1,0:T(8,128)(2,1)S(1)}, u32[]{:S(2)}, u32[]{:S(2)}) collective-permute-start(bf16[2048,128]{1,0:T(8,128)(2,1)S(1)} %constant_dynamic-update-slice_fusion.25.refs_1_.refs_3_), channel_id=1, source_target_pairs={{0,1},{1,0},{2,3},{3,2},{4,5},{5,4},{6,7},{7,6},{8,9},{9,8},{10,11... | collective-permute-start | bytes 1572872 | tf_op jit(solution)/shard_map/ppermute | solution.py:31
  35.0 7.0 %collective-permute-start.11 = (bf16[1536,128]{1,0:T(8,128)(2,1)S(1)}, bf16[1536,128]{1,0:T(8,128)(2,1)S(1)}, u32[]{:S(2)}, u32[]{:S(2)}) collective-permute-start(bf16[1536,128]{1,0:T(8,128)(2,1)S(1)} %constant_dynamic-update-slice_fusion.36.refs_4_), channel_id=1, source_target_pairs={{0,1},{1,0},{2,3},{3,2},{4,5},{5,4},{6,7},{7,6},{8,9},{9,8},{10,11... | collective-permute-start | bytes 1179656 | tf_op jit(solution)/shard_map/ppermute | solution.py:31
  35.1 1.9 %collective-permute-start.16 = (bf16[512,128]{1,0:T(8,128)(2,1)S(1)}, bf16[512,128]{1,0:T(8,128)(2,1)S(1)}, u32[]{:S(2)}, u32[]{:S(2)}) collective-permute-start(bf16[512,128]{1,0:T(8,128)(2,1)S(1)} %constant_dynamic-update-slice_fusion.8.refs_0_.refs_4_), channel_id=1, source_target_pairs={{0,1},{1,0},{2,3},{3,2},{4,5},{5,4},{6,7},{7,6},{8,9},{9,8},{10,11... | collective-permute-start | bytes 393224 | tf_op jit(solution)/shard_map/ppermute | solution.py:31
  42.0 10.8 %collective-permute-start.12 = (f16[288,128]{1,0:T(8,128)(2,1)S(1)}, f16[288,128]{1,0:T(8,128)(2,1)S(1)}, u32[]{:S(2)}, u32[]{:S(2)}) collective-permute-start(f16[288,128]{1,0:T(8,128)(2,1)S(1)} %convert_element_type.73), channel_id=1, source_target_pairs={{0,64},{64,0},{128,192},{192,128},{1,65},{65,1},{129,193},{193,129... | collective-permute-start | bytes 221192 | tf_op jit(solution)/shard_map/ppermute | solution.py:31
  42.7 11.0 %collective-permute-start.13 = (f16[288,128]{1,0:T(8,128)(2,1)S(1)}, f16[288,128]{1,0:T(8,128)(2,1)S(1)}, u32[]{:S(2)}, u32[]{:S(2)}) collective-permute-start(f16[288,128]{1,0:T(8,128)(2,1)S(1)} %convert_element_type.74), channel_id=1, source_target_pairs={{0,128},{64,192},{128,0},{192,64},{1,129},{65,193},{129,1},{193,65... | collective-permute-start | bytes 221192 | tf_op jit(solution)/shard_map/ppermute | solution.py:31
  45.6 8.2 %collective-permute-start.14 = (f16[288,128]{1,0:T(8,128)(2,1)S(1)}, f16[288,128]{1,0:T(8,128)(2,1)S(1)}, u32[]{:S(2)}, u32[]{:S(2)}) collective-permute-start(f16[288,128]{1,0:T(8,128)(2,1)S(1)} %convert_element_type.75), channel_id=1, source_target_pairs={{0,192},{64,128},{128,64},{192,0},{1,193},{65,129},{129,65},{193,1... | collective-permute-start | bytes 221192 | tf_op jit(solution)/shard_map/ppermute | solution.py:31
  49.5 5.5 %collective-permute-start.19 = (f16[288,128]{1,0:T(8,128)(2,1)S(1)}, f16[288,128]{1,0:T(8,128)(2,1)S(1)}, u32[]{:S(2)}, u32[]{:S(2)}) collective-permute-start(f16[288,128]{1,0:T(8,128)(2,1)S(1)} %convert_element_type.88), channel_id=1, source_target_pairs={{0,12},{4,8},{8,4},{12,0},{1,13},{5,9},{9,5},{13,1},{2,14},{6,10},... | collective-permute-start | bytes 221192 | tf_op jit(solution)/shard_map/ppermute | solution.py:31
  50.1 5.9 %collective-permute-start.18 = (f16[288,128]{1,0:T(8,128)(2,1)S(1)}, f16[288,128]{1,0:T(8,128)(2,1)S(1)}, u32[]{:S(2)}, u32[]{:S(2)}) collective-permute-start(f16[288,128]{1,0:T(8,128)(2,1)S(1)} %convert_element_type.86), channel_id=1, source_target_pairs={{0,8},{4,12},{8,0},{12,4},{1,9},{5,13},{9,1},{13,5},{2,10},{6,14},... | collective-permute-start | bytes 221192 | tf_op jit(solution)/shard_map/ppermute | solution.py:31
  52.9 4.4 %collective-permute-start.17 = (f16[288,128]{1,0:T(8,128)(2,1)S(1)}, f16[288,128]{1,0:T(8,128)(2,1)S(1)}, u32[]{:S(2)}, u32[]{:S(2)}) collective-permute-start(f16[288,128]{1,0:T(8,128)(2,1)S(1)} %convert_element_type.84), channel_id=1, source_target_pairs={{0,4},{4,0},{8,12},{12,8},{1,5},{5,1},{9,13},{13,9},{2,6},{6,2},{1... | collective-permute-start | bytes 221192 | tf_op jit(solution)/shard_map/ppermute | solution.py:31
  54.0 4.0 %collective-permute-start.15 = (f16[144,128]{1,0:T(8,128)(2,1)S(1)}, f16[144,128]{1,0:T(8,128)(2,1)S(1)}, u32[]{:S(2)}, u32[]{:S(2)}) collective-permute-start(f16[144,128]{1,0:T(8,128)(2,1)S(1)} %convert_element_type.80), channel_id=1, source_target_pairs={{0,2},{2,0},{1,3},{3,1},{4,6},{6,4},{5,7},{7,5},{8,10},{10,8},{9,1... | collective-permute-start | bytes 110600 | tf_op jit(solution)/shard_map/ppermute | solution.py:31
  58.4 6.6 %collective-permute-start.22 = (f16[96,128]{1,0:T(8,128)(2,1)S(1)}, f16[96,128]{1,0:T(8,128)(2,1)S(1)}, u32[]{:S(2)}, u32[]{:S(2)}) collective-permute-start(f16[96,128]{1,0:T(8,128)(2,1)S(1)} %convert_element_type.94), channel_id=1, source_target_pairs={{0,48},{16,32},{32,16},{48,0},{1,49},{17,33},{33,17},{49,1},{2,50}... | collective-permute-start | bytes 73736 | tf_op jit(solution)/shard_map/ppermute | solution.py:31
  60.7 7.7 %collective-permute-start.21 = (f16[96,128]{1,0:T(8,128)(2,1)S(1)}, f16[96,128]{1,0:T(8,128)(2,1)S(1)}, u32[]{:S(2)}, u32[]{:S(2)}) collective-permute-start(f16[96,128]{1,0:T(8,128)(2,1)S(1)} %convert_element_type.92), channel_id=1, source_target_pairs={{0,32},{16,48},{32,0},{48,16},{1,33},{17,49},{33,1},{49,17},{2,34}... | collective-permute-start | bytes 73736 | tf_op jit(solution)/shard_map/ppermute | solution.py:31
  63.4 5.0 %collective-permute-start.20 = (f16[96,128]{1,0:T(8,128)(2,1)S(1)}, f16[96,128]{1,0:T(8,128)(2,1)S(1)}, u32[]{:S(2)}, u32[]{:S(2)}) collective-permute-start(f16[96,128]{1,0:T(8,128)(2,1)S(1)} %convert_element_type.90), channel_id=1, source_target_pairs={{0,16},{16,0},{32,48},{48,32},{1,17},{17,1},{33,49},{49,33},{2,18}... | collective-permute-start | bytes 73736 | tf_op jit(solution)/shard_map/ppermute | solution.py:31

commit v2 on v1

--- a/solution.py
+++ b/solution.py
@@ -20,6 +20,7 @@
 SMEM = pl.BlockSpec(memory_space=pltpu.SMEM)
 HBM = pl.BlockSpec(memory_space=pltpu.HBM)
 GROUP = 256
+CHUNK_A = 1024
 PARAMS = pltpu.CompilerParams(vmem_limit_bytes=24 * 1024 * 1024)
 SMALL = pltpu.CompilerParams(vmem_limit_bytes=8 * 1024 * 1024)
 
@@ -32,7 +33,10 @@
 
 
 def exchange(blocks, axes):
-    return [blocks[0]] + [swap(b, axes, k) for k, b in enumerate(blocks) if k]
+    taken = [blocks[0]]
+    for k, block in enumerate(blocks[1:], 1):
+        taken.append(swap(block, axes, k))
+    return taken
 
 
 def gather(block, axes):
@@ -83,24 +87,25 @@
     return parts[0] if len(parts) == 1 else jnp.concatenate(parts)
 
 
-def attend_kernel(rows, span, n_q, n_kv, carried, final, *refs):
+def attend_kernel(rows, span, chunk_keys, n_q, n_kv, carried, final, *refs):
     q_refs, kv_refs = refs[:n_q], refs[n_q : n_q + n_kv]
     before = refs[n_q + n_kv : n_q + n_kv + 2 * carried]
     outs, scores = refs[n_q + n_kv + 2 * carried : -1], refs[-1]
     keys = [(ref, at) for ref in kv_refs for at in range(0, ref.shape[0], 2 * span)]
     blocks = [(i, j) for i, ref in enumerate(q_refs) for j in range(ref.shape[0] // (2 * rows))]
     step = GROUP // rows
+    per = chunk_keys // span
+    keys = [keys[n : n + per] for n in range(0, len(keys), per)]
+    starts = [n * chunk_keys for n in range(len(keys))]
     groups = [blocks[g : g + step] for g in range(0, len(blocks), step)]
     tops = [None] * len(groups)
 
     def score(g, n):
         queries = joined([q_refs[i][2 * rows * j : 2 * rows * j + rows, :] for i, j in groups[g]])
-        ref, at = keys[n]
-        logits = lax.dot_general(
-            queries, ref[at : at + span, :], (((1,), (1,)), ((), ())), preferred_element_type=jnp.float32
-        )
-        scores[g % 2, : queries.shape[0], n * span : (n + 1) * span] = logits
-        for c in range(0, span, LANES):
+        piece = joined([ref[at : at + span, :] for ref, at in keys[n]])
+        logits = lax.dot_general(queries, piece, (((1,), (1,)), ((), ())), preferred_element_type=jnp.float32)
+        scores[g % 2, : queries.shape[0], starts[n] : starts[n] + logits.shape[1]] = logits
+        for c in range(0, logits.shape[1], LANES):
             part = logits[:, c : c + LANES]
             tops[g] = part if tops[g] is None else jnp.maximum(tops[g], part)
 
@@ -110,14 +115,13 @@
         g, size = at_group * step, rows * len(group)
         peak = jnp.max(tops[at_group], axis=1, keepdims=True) * SCALE
         total, number = None, None
-        for n, (ref, at) in enumerate(keys):
-            weights = jnp.exp2(scores[at_group % 2, :size, n * span : (n + 1) * span] * SCALE - peak)
-            for c in range(0, span, LANES):
+        for n, chunk in enumerate(keys):
+            piece = joined([ref[at + span : at + 2 * span, :] for ref, at in chunk])
+            weights = jnp.exp2(scores[at_group % 2, :size, starts[n] : starts[n] + piece.shape[0]] * SCALE - peak)
+            for c in range(0, piece.shape[0], LANES):
                 part = weights[:, c : c + LANES]
                 total = part if total is None else total + part
-            part = jnp.dot(
-                weights.astype(jnp.bfloat16), ref[at + span : at + 2 * span, :], preferred_element_type=jnp.float32
-            )
+            part = jnp.dot(weights.astype(jnp.bfloat16), piece, preferred_element_type=jnp.float32)
             number = part if number is None else number + part
             if at_group + 1 < len(groups):
                 score(at_group + 1, n)
@@ -145,7 +149,7 @@
                 )
 
 
-def attention(rows, q_blocks, span, kv_stacks, before=(), final=True):
+def attention(rows, q_blocks, span, kv_stacks, before=(), final=True, chunk=None):
     heights = [q.shape[0] // 2 for q in q_blocks]
     whole = sum(heights)
     keys = sum(s.shape[0] for s in kv_stacks) // 2
@@ -155,7 +159,7 @@
         shapes = [(whole, HEAD), (whole, LANES)]
     n_q, n_kv = len(q_blocks), len(kv_stacks)
     return pl.pallas_call(
-        functools.partial(attend_kernel, rows, span, n_q, n_kv, len(before) // 2, final),
+        functools.partial(attend_kernel, rows, span, chunk or span, n_q, n_kv, len(before) // 2, final),
         out_shape=[jax.ShapeDtypeStruct(s, jnp.float32) for s in shapes],
         in_specs=[VMEM] * (n_q + n_kv + len(before)),
         out_specs=[VMEM] * len(shapes),
@@ -242,9 +246,9 @@
     other_a = swap(rest_a, CORE, 1)
 
     keys_b = [all_b, other_b]
-    part_a = attention(span_a, pairs_a[:1], span_b, keys_b)
+    part_a = attention(span_a, pairs_a[:1], span_b, keys_b, chunk=CHUNK_A)
     begun = attention(span_b, blocks_b, span_a, [pair_a, first_a], final=False)
-    part_a += attention(span_a, pairs_a[1:], span_b, keys_b)
+    part_a += attention(span_a, pairs_a[1:], span_b, keys_b, chunk=CHUNK_A)
     part_a = [p.astype(f16) for p in part_a]
     part_a, other_a = lax.optimization_barrier((part_a, other_a))
     part_b = attention(span_b, blocks_b, span_a, [rest_a, other_a], before=begun)
@@ -271,7 +275,8 @@
         out_specs=[VMEM] * heads,
         compiler_params=SMALL,
     )(*part_a, *part_b)
-    back = [done[0]] + [b.astype(f32) for b in exchange([d.astype(f16) for d in done], HEAD_AXIS)[1:]]
+    back = exchange([d.astype(f16) for d in done], HEAD_AXIS)
+    back = [done[0]] + [b.astype(f32) for b in back[1:]]
     return pl.pallas_call(
         join_heads,
         out_shape=[

time: 69.3 us -> 69.1 us (level)
  no operation moved by 1% of the time
where the time goes in v2:
time: 69.1 us; the launch traced here: 68.9 us
  starting transfers between devices  35.4 us (51%)
  waiting for transfers between devices  22.4 us (32%)
  Pallas kernels  9.52 us (14%)
  between operations  0.99 us (1%)
    ppermute x23, starting transfers between devices, swap(): return lax.ppermute(value, axes, [(i, i ^ k) for i in range(size)])  35.4 us
    ppermute x23, waiting for transfers between devices, swap(): return lax.ppermute(value, axes, [(i, i ^ k) for i in range(size)])  22.4 us
    pallas_call x4, Pallas kernels, attention(): pl.pallas_call(functools.partial(attend_kernel, rows, span, chunk or span...  7.29 us
  transfers between devices with their start and end apart: 23, of which 10 were waited for; matrix products, arithmetic and copies ran while one was open for 1% of the time, Pallas kernels for 11%

profile of v2, /device:TPU:4, one launch (start us, length us, event | category | flops | bytes accessed | tf_op | source)
XLA Modules:
  0.0 68.9 jit_solution(17815455226130265407)
XLA Ops:
  0.6 1.0 %shard_map.59 = (bf16[192,128]{1,0:T(8,128)(2,1)S(1)}, bf16[192,128]{1,0:T(8,128)(2,1)S(1)}, bf16[192,128]{1,0:T(8,128)(2,1)S(1)}, bf16[192,128]{1,0:T(8,128)(2,1)S(1)}) custom-call(s32[1]{0:T(128)} %bitcast.place, bf16[32,512]{1,0:T(8,128)(2,1)} %refs_0_.1, bf16[32,512]{1,0:T(8,128)(2,1)} %refs_1_.1, bf16[64,512]{1,0:T(8,128)(2,1)} %refs_2_.1, ...), custom_call_target="tpu_custom_call" | custom-call | tf_op jit(solution)/shard_map/pallas_call | solution.py:224
  1.7 3.4 %collective-permute-start = (bf16[192,128]{1,0:T(8,128)(2,1)S(1)}, bf16[192,128]{1,0:T(8,128)(2,1)S(1)}, u32[]{:S(2)}, u32[]{:S(2)}) collective-permute-start(bf16[192,128]{1,0:T(8,128)(2,1)S(1)} %get-tuple-element.25), channel_id=1, source_target_pairs={{0,16},{16,0},{32,48},{48,32},{1,17},{17,1},{33,49},{49,33},{2,18}... | collective-permute-start | bytes 147464 | tf_op jit(solution)/shard_map/ppermute | solution.py:32
  5.0 5.4 %collective-permute-start.1 = (bf16[192,128]{1,0:T(8,128)(2,1)S(1)}, bf16[192,128]{1,0:T(8,128)(2,1)S(1)}, u32[]{:S(2)}, u32[]{:S(2)}) collective-permute-start(bf16[192,128]{1,0:T(8,128)(2,1)S(1)} %get-tuple-element.26), channel_id=1, source_target_pairs={{0,32},{16,48},{32,0},{48,16},{1,33},{17,49},{33,1},{49,17},{2,34}... | collective-permute-start | bytes 147464 | tf_op jit(solution)/shard_map/ppermute | solution.py:32
  10.5 2.6 %collective-permute-done.1 = bf16[192,128]{1,0:T(8,128)(2,1)S(1)} collective-permute-done((bf16[192,128]{1,0:T(8,128)(2,1)S(1)}, bf16[192,128]{1,0:T(8,128)(2,1)S(1)}, u32[]{:S(2)}, u32[]{:S(2)}) %collective-permute-start.1) | collective-permute-done | bytes 49184 | tf_op jit(solution)/shard_map/ppermute | solution.py:32
  13.0 3.7 %collective-permute-done.2 = bf16[192,128]{1,0:T(8,128)(2,1)S(1)} collective-permute-done((bf16[192,128]{1,0:T(8,128)(2,1)S(1)}, bf16[192,128]{1,0:T(8,128)(2,1)S(1)}, u32[]{:S(2)}, u32[]{:S(2)}) %collective-permute-start.2) | collective-permute-done | bytes 49184 | tf_op jit(solution)/shard_map/ppermute | solution.py:32
  17.4 2.7 %collective-permute-start.5 = (bf16[512,128]{1,0:T(8,128)(2,1)S(1)}, bf16[512,128]{1,0:T(8,128)(2,1)S(1)}, u32[]{:S(2)}, u32[]{:S(2)}) collective-permute-start(bf16[512,128]{1,0:T(8,128)(2,1)S(1)} %get-tuple-element.46.refs_0_), channel_id=1, source_target_pairs={{0,8},{4,12},{8,0},{12,4},{1,9},{5,13},{9,1},{13,5},{2,10},{6,14},... | collective-permute-start | bytes 393224 | tf_op jit(solution)/shard_map/ppermute | solution.py:32
  20.1 0.8 %collective-permute-start.4 = (bf16[512,128]{1,0:T(8,128)(2,1)S(1)}, bf16[512,128]{1,0:T(8,128)(2,1)S(1)}, u32[]{:S(2)}, u32[]{:S(2)}) collective-permute-start(bf16[512,128]{1,0:T(8,128)(2,1)S(1)} %get-tuple-element.46.refs_0_), channel_id=1, source_target_pairs={{0,4},{4,0},{8,12},{12,8},{1,5},{5,1},{9,13},{13,9},{2,6},{6,2},{1... | collective-permute-start | bytes 393224 | tf_op jit(solution)/shard_map/ppermute | solution.py:32
  21.0 1.0 %collective-permute-start.3 = (bf16[256,128]{1,0:T(8,128)(2,1)S(1)}, bf16[256,128]{1,0:T(8,128)(2,1)S(1)}, u32[]{:S(2)}, u32[]{:S(2)}) collective-permute-start(bf16[256,128]{1,0:T(8,128)(2,1)S(1)} %get-tuple-element.54), channel_id=1, source_target_pairs={{0,2},{2,0},{1,3},{3,1},{4,6},{6,4},{5,7},{7,5},{8,10},{10,8},{9,1... | collective-permute-start | bytes 196616 | tf_op jit(solution)/shard_map/ppermute | solution.py:32
  22.1 3.2 %collective-permute-done.3 = bf16[256,128]{1,0:T(8,128)(2,1)S(1)} collective-permute-done((bf16[256,128]{1,0:T(8,128)(2,1)S(1)}, bf16[256,128]{1,0:T(8,128)(2,1)S(1)}, u32[]{:S(2)}, u32[]{:S(2)}) %collective-permute-start.3) | collective-permute-done | bytes 65568 | tf_op jit(solution)/shard_map/ppermute | solution.py:32
  25.4 3.1 %collective-permute-start.10 = (bf16[512,128]{1,0:T(8,128)(2,1)S(1)}, bf16[512,128]{1,0:T(8,128)(2,1)S(1)}, u32[]{:S(2)}, u32[]{:S(2)}) collective-permute-start(bf16[512,128]{1,0:T(8,128)(2,1)S(1)} %constant_dynamic-update-slice_fusion.8.refs_0_.refs_4_), channel_id=1, source_target_pairs={{0,192},{64,128},{128,64},{192,0},{1,193},{65,129},{129,65},{193,1... | collective-permute-start | bytes 393224 | tf_op jit(solution)/shard_map/ppermute | solution.py:32
  28.5 0.6 collective-permute-start.9
  29.8 4.3 %collective-permute-done.8.refs_0_ = bf16[512,128]{1,0:T(8,128)(2,1)S(1)} collective-permute-done((bf16[512,128]{1,0:T(8,128)(2,1)S(1)}, bf16[512,128]{1,0:T(8,128)(2,1)S(1)}, u32[]{:S(2)}, u32[]{:S(2)}) %collective-permute-start.8) | collective-permute-done | bytes 131104 | tf_op jit(solution)/shard_map/ppermute | solution.py:32
  34.1 0.9 %collective-permute-done.9.refs_1_ = bf16[512,128]{1,0:T(8,128)(2,1)S(1)} collective-permute-done((bf16[512,128]{1,0:T(8,128)(2,1)S(1)}, bf16[512,128]{1,0:T(8,128)(2,1)S(1)}, u32[]{:S(2)}, u32[]{:S(2)}) %collective-permute-start.9) | collective-permute-done | bytes 131104 | tf_op jit(solution)/shard_map/ppermute | solution.py:32
  35.6 1.4 %collective-permute-done.16.refs_5_ = bf16[512,128]{1,0:T(8,128)(2,1)S(1)} collective-permute-done((bf16[512,128]{1,0:T(8,128)(2,1)S(1)}, bf16[512,128]{1,0:T(8,128)(2,1)S(1)}, u32[]{:S(2)}, u32[]{:S(2)}) %collective-permute-start.16) | collective-permute-done | bytes 131104 | tf_op jit(solution)/shard_map/ppermute | solution.py:32
  37.0 1.1 %shard_map.63 = (f32[1024,128]{1,0:T(8,128)S(1)}, f32[1024,128]{1,0:T(8,128)S(1)}) custom-call(bf16[512,128]{1,0:T(8,128)(2,1)S(1)} %get-tuple-element.46.refs_0_, bf16[512,128]{1,0:T(8,128)(2,1)S(1)} %collective-permute-done.4.refs_1_, bf16[512,128]{1,0:T(8,128)(2,1)S(1)} %collective-permute-done.5.refs_2_, ...), custom_call_target="tpu_custom_call" | custom-call | flops 268435456 | tf_op jit(solution)/shard_map/pallas_call | solution.py:161
  38.1 1.1 %shard_map.60 = f32[288,128]{1,0:T(8,128)S(1)} custom-call(bf16[512,128]{1,0:T(8,128)(2,1)S(1)} %constant_dynamic-update-slice_fusion.8.refs_0_.refs_4_, bf16[2048,128]{1,0:T(8,128)(2,1)S(1)} %constant_dynamic-update-slice_fusion.25.refs_1_.refs_3_, bf16[2048,128]{1,0:T(8,128)(2,1)S(1)} %collective-permute-done.7.refs_2_.refs_4_), custom_call_target="tpu_custom_call" | custom-call | flops 268435456 | tf_op jit(solution)/shard_map/pallas_call | solution.py:161
  39.2 2.5 %shard_map.61 = (f32[288,128]{1,0:T(8,128)S(1)}, f32[288,128]{1,0:T(8,128)S(1)}, f32[288,128]{1,0:T(8,128)S(1)}) custom-call(bf16[512,128]{1,0:T(8,128)(2,1)S(1)} %collective-permute-done.8.refs_0_, bf16[512,128]{1,0:T(8,128)(2,1)S(1)} %collective-permute-done.9.refs_1_, bf16[512,128]{1,0:T(8,128)(2,1)S(1)} %collective-permute-done.10.refs_2_, ...), custom_call_target="tpu_custom_call" | custom-call | flops 805306368 | tf_op jit(solution)/shard_map/pallas_call | solution.py:161
  41.8 0.6 collective-permute-start.12
  42.5 2.9 %collective-permute-start.13 = (f16[288,128]{1,0:T(8,128)(2,1)S(1)}, f16[288,128]{1,0:T(8,128)(2,1)S(1)}, u32[]{:S(2)}, u32[]{:S(2)}) collective-permute-start(f16[288,128]{1,0:T(8,128)(2,1)S(1)} %convert_element_type.74), channel_id=1, source_target_pairs={{0,128},{64,192},{128,0},{192,64},{1,129},{65,193},{129,1},{193,65... | collective-permute-start | bytes 221192 | tf_op jit(solution)/shard_map/ppermute | solution.py:32
  45.4 1.2 %collective-permute-start.14 = (f16[288,128]{1,0:T(8,128)(2,1)S(1)}, f16[288,128]{1,0:T(8,128)(2,1)S(1)}, u32[]{:S(2)}, u32[]{:S(2)}) collective-permute-start(f16[288,128]{1,0:T(8,128)(2,1)S(1)} %convert_element_type.75), channel_id=1, source_target_pairs={{0,192},{64,128},{128,64},{192,0},{1,193},{65,129},{129,65},{193,1... | collective-permute-start | bytes 221192 | tf_op jit(solution)/shard_map/ppermute | solution.py:32
  46.6 2.6 %shard_map.64 = (f32[288,128]{1,0:T(8,128)S(1)}, f32[288,128]{1,0:T(8,128)S(1)}, f32[288,128]{1,0:T(8,128)S(1)}, f32[288,128]{1,0:T(8,128)S(1)}) custom-call(bf16[512,128]{1,0:T(8,128)(2,1)S(1)} %get-tuple-element.46.refs_0_, bf16[512,128]{1,0:T(8,128)(2,1)S(1)} %collective-permute-done.4.refs_1_, bf16[512,128]{1,0:T(8,128)(2,1)S(1)} %collective-permute-done.5.refs_2_, ...), custom_call_target="tpu_custom_call" | custom-call | flops 805306368 | tf_op jit(solution)/shard_map/pallas_call | solution.py:161
  49.9 2.7 %collective-permute-start.18 = (f16[288,128]{1,0:T(8,128)(2,1)S(1)}, f16[288,128]{1,0:T(8,128)(2,1)S(1)}, u32[]{:S(2)}, u32[]{:S(2)}) collective-permute-start(f16[288,128]{1,0:T(8,128)(2,1)S(1)} %convert_element_type.86), channel_id=1, source_target_pairs={{0,8},{4,12},{8,0},{12,4},{1,9},{5,13},{9,1},{13,5},{2,10},{6,14},... | collective-permute-start | bytes 221192 | tf_op jit(solution)/shard_map/ppermute | solution.py:32
  52.7 0.8 %collective-permute-start.17 = (f16[288,128]{1,0:T(8,128)(2,1)S(1)}, f16[288,128]{1,0:T(8,128)(2,1)S(1)}, u32[]{:S(2)}, u32[]{:S(2)}) collective-permute-start(f16[288,128]{1,0:T(8,128)(2,1)S(1)} %convert_element_type.84), channel_id=1, source_target_pairs={{0,4},{4,0},{8,12},{12,8},{1,5},{5,1},{9,13},{13,9},{2,6},{6,2},{1... | collective-permute-start | bytes 221192 | tf_op jit(solution)/shard_map/ppermute | solution.py:32
  53.8 1.0 %collective-permute-start.15 = (f16[144,128]{1,0:T(8,128)(2,1)S(1)}, f16[144,128]{1,0:T(8,128)(2,1)S(1)}, u32[]{:S(2)}, u32[]{:S(2)}) collective-permute-start(f16[144,128]{1,0:T(8,128)(2,1)S(1)} %convert_element_type.80), channel_id=1, source_target_pairs={{0,2},{2,0},{1,3},{3,1},{4,6},{6,4},{5,7},{7,5},{8,10},{10,8},{9,1... | collective-permute-start | bytes 110600 | tf_op jit(solution)/shard_map/ppermute | solution.py:32
  54.8 1.0 %collective-permute-done.18 = f16[288,128]{1,0:T(8,128)(2,1)S(1)} collective-permute-done((f16[288,128]{1,0:T(8,128)(2,1)S(1)}, f16[288,128]{1,0:T(8,128)(2,1)S(1)}, u32[]{:S(2)}, u32[]{:S(2)}) %collective-permute-start.18) | collective-permute-done | bytes 73760 | tf_op jit(solution)/shard_map/ppermute | solution.py:32
  55.8 1.2 %collective-permute-done.17 = f16[288,128]{1,0:T(8,128)(2,1)S(1)} collective-permute-done((f16[288,128]{1,0:T(8,128)(2,1)S(1)}, f16[288,128]{1,0:T(8,128)(2,1)S(1)}, u32[]{:S(2)}, u32[]{:S(2)}) %collective-permute-start.17) | collective-permute-done | bytes 73760 | tf_op jit(solution)/shard_map/ppermute | solution.py:32
  57.0 0.8 %collective-permute-done.15 = f16[144,128]{1,0:T(8,128)(2,1)S(1)} collective-permute-done((f16[144,128]{1,0:T(8,128)(2,1)S(1)}, f16[144,128]{1,0:T(8,128)(2,1)S(1)}, u32[]{:S(2)}, u32[]{:S(2)}) %collective-permute-start.15) | collective-permute-done | bytes 36896 | tf_op jit(solution)/shard_map/ppermute | solution.py:32
  58.2 2.3 %collective-permute-start.22 = (f16[96,128]{1,0:T(8,128)(2,1)S(1)}, f16[96,128]{1,0:T(8,128)(2,1)S(1)}, u32[]{:S(2)}, u32[]{:S(2)}) collective-permute-start(f16[96,128]{1,0:T(8,128)(2,1)S(1)} %convert_element_type.94), channel_id=1, source_target_pairs={{0,48},{16,32},{32,16},{48,0},{1,49},{17,33},{33,17},{49,1},{2,50}... | collective-permute-start | bytes 73736 | tf_op jit(solution)/shard_map/ppermute | solution.py:32
  60.5 2.8 %collective-permute-start.21 = (f16[96,128]{1,0:T(8,128)(2,1)S(1)}, f16[96,128]{1,0:T(8,128)(2,1)S(1)}, u32[]{:S(2)}, u32[]{:S(2)}) collective-permute-start(f16[96,128]{1,0:T(8,128)(2,1)S(1)} %convert_element_type.92), channel_id=1, source_target_pairs={{0,32},{16,48},{32,0},{48,16},{1,33},{17,49},{33,1},{49,17},{2,34}... | collective-permute-start | bytes 73736 | tf_op jit(solution)/shard_map/ppermute | solution.py:32
  63.2 1.5 %collective-permute-start.20 = (f16[96,128]{1,0:T(8,128)(2,1)S(1)}, f16[96,128]{1,0:T(8,128)(2,1)S(1)}, u32[]{:S(2)}, u32[]{:S(2)}) collective-permute-start(f16[96,128]{1,0:T(8,128)(2,1)S(1)} %convert_element_type.90), channel_id=1, source_target_pairs={{0,16},{16,0},{32,48},{48,32},{1,17},{17,1},{33,49},{49,33},{2,18}... | collective-permute-start | bytes 73736 | tf_op jit(solution)/shard_map/ppermute | solution.py:32
  64.8 3.4 %collective-permute-done.21 = f16[96,128]{1,0:T(8,128)(2,1)S(1)} collective-permute-done((f16[96,128]{1,0:T(8,128)(2,1)S(1)}, f16[96,128]{1,0:T(8,128)(2,1)S(1)}, u32[]{:S(2)}, u32[]{:S(2)}) %collective-permute-start.21) | collective-permute-done | bytes 24608 | tf_op jit(solution)/shard_map/ppermute | solution.py:32
  68.2 0.7 %shard_map.66 = (f32[32,512]{1,0:T(8,128)}, f32[64,512]{1,0:T(8,128)}) custom-call(s32[1]{0:T(128)} %bitcast.place, f32[96,128]{1,0:T(8,128)S(1)} %get-tuple-element.42.refs_0_, f32[96,128]{1,0:T(8,128)S(1)} %convert_element_type.91.refs_1_, f32[96,128]{1,0:T(8,128)S(1)} %convert_element_type.93.refs_2_, f32[96,128]{1,0:T(8,128)S(1)} %convert_element_type.95.refs_3_), custom_call_target="tpu_custom_call" | custom-call | tf_op jit(solution)/shard_map/pallas_call | solution.py:280
  (76 shorter events, 3.5 us)
Async XLA Ops:
  1.7 8.8 %collective-permute-start = (bf16[192,128]{1,0:T(8,128)(2,1)S(1)}, bf16[192,128]{1,0:T(8,128)(2,1)S(1)}, u32[]{:S(2)}, u32[]{:S(2)}) collective-permute-start(bf16[192,128]{1,0:T(8,128)(2,1)S(1)} %get-tuple-element.25), channel_id=1, source_target_pairs={{0,16},{16,0},{32,48},{48,32},{1,17},{17,1},{33,49},{49,33},{2,18}... | collective-permute-start | bytes 147464 | tf_op jit(solution)/shard_map/ppermute | solution.py:32
  5.0 8.0 %collective-permute-start.1 = (bf16[192,128]{1,0:T(8,128)(2,1)S(1)}, bf16[192,128]{1,0:T(8,128)(2,1)S(1)}, u32[]{:S(2)}, u32[]{:S(2)}) collective-permute-start(bf16[192,128]{1,0:T(8,128)(2,1)S(1)} %get-tuple-element.26), channel_id=1, source_target_pairs={{0,32},{16,48},{32,0},{48,16},{1,33},{17,49},{33,1},{49,17},{2,34}... | collective-permute-start | bytes 147464 | tf_op jit(solution)/shard_map/ppermute | solution.py:32
  10.4 6.3 %collective-permute-start.2 = (bf16[192,128]{1,0:T(8,128)(2,1)S(1)}, bf16[192,128]{1,0:T(8,128)(2,1)S(1)}, u32[]{:S(2)}, u32[]{:S(2)}) collective-permute-start(bf16[192,128]{1,0:T(8,128)(2,1)S(1)} %get-tuple-element.27), channel_id=1, source_target_pairs={{0,48},{16,32},{32,16},{48,0},{1,49},{17,33},{33,17},{49,1},{2,50}... | collective-permute-start | bytes 147464 | tf_op jit(solution)/shard_map/ppermute | solution.py:32
  16.8 12.9 %collective-permute-start.6 = (bf16[512,128]{1,0:T(8,128)(2,1)S(1)}, bf16[512,128]{1,0:T(8,128)(2,1)S(1)}, u32[]{:S(2)}, u32[]{:S(2)}) collective-permute-start(bf16[512,128]{1,0:T(8,128)(2,1)S(1)} %get-tuple-element.46.refs_0_), channel_id=1, source_target_pairs={{0,12},{4,8},{8,4},{12,0},{1,13},{5,9},{9,5},{13,1},{2,14},{6,10},... | collective-permute-start | bytes 393224 | tf_op jit(solution)/shard_map/ppermute | solution.py:32
  17.4 12.2 %collective-permute-start.5 = (bf16[512,128]{1,0:T(8,128)(2,1)S(1)}, bf16[512,128]{1,0:T(8,128)(2,1)S(1)}, u32[]{:S(2)}, u32[]{:S(2)}) collective-permute-start(bf16[512,128]{1,0:T(8,128)(2,1)S(1)} %get-tuple-element.46.refs_0_), channel_id=1, source_target_pairs={{0,8},{4,12},{8,0},{12,4},{1,9},{5,13},{9,1},{13,5},{2,10},{6,14},... | collective-permute-start | bytes 393224 | tf_op jit(solution)/shard_map/ppermute | solution.py:32
  20.1 9.0 %collective-permute-start.4 = (bf16[512,128]{1,0:T(8,128)(2,1)S(1)}, bf16[512,128]{1,0:T(8,128)(2,1)S(1)}, u32[]{:S(2)}, u32[]{:S(2)}) collective-permute-start(bf16[512,128]{1,0:T(8,128)(2,1)S(1)} %get-tuple-element.46.refs_0_), channel_id=1, source_target_pairs={{0,4},{4,0},{8,12},{12,8},{1,5},{5,1},{9,13},{13,9},{2,6},{6,2},{1... | collective-permute-start | bytes 393224 | tf_op jit(solution)/shard_map/ppermute | solution.py:32
  21.0 4.4 %collective-permute-start.3 = (bf16[256,128]{1,0:T(8,128)(2,1)S(1)}, bf16[256,128]{1,0:T(8,128)(2,1)S(1)}, u32[]{:S(2)}, u32[]{:S(2)}) collective-permute-start(bf16[256,128]{1,0:T(8,128)(2,1)S(1)} %get-tuple-element.54), channel_id=1, source_target_pairs={{0,2},{2,0},{1,3},{3,1},{4,6},{6,4},{5,7},{7,5},{8,10},{10,8},{9,1... | collective-permute-start | bytes 196616 | tf_op jit(solution)/shard_map/ppermute | solution.py:32
  25.4 9.6 %collective-permute-start.10 = (bf16[512,128]{1,0:T(8,128)(2,1)S(1)}, bf16[512,128]{1,0:T(8,128)(2,1)S(1)}, u32[]{:S(2)}, u32[]{:S(2)}) collective-permute-start(bf16[512,128]{1,0:T(8,128)(2,1)S(1)} %constant_dynamic-update-slice_fusion.8.refs_0_.refs_4_), channel_id=1, source_target_pairs={{0,192},{64,128},{128,64},{192,0},{1,193},{65,129},{129,65},{193,1... | collective-permute-start | bytes 393224 | tf_op jit(solution)/shard_map/ppermute | solution.py:32
  28.5 6.5 %collective-permute-start.9 = (bf16[512,128]{1,0:T(8,128)(2,1)S(1)}, bf16[512,128]{1,0:T(8,128)(2,1)S(1)}, u32[]{:S(2)}, u32[]{:S(2)}) collective-permute-start(bf16[512,128]{1,0:T(8,128)(2,1)S(1)} %constant_dynamic-update-slice_fusion.8.refs_0_.refs_4_), channel_id=1, source_target_pairs={{0,128},{64,192},{128,0},{192,64},{1,129},{65,193},{129,1},{193,65... | collective-permute-start | bytes 393224 | tf_op jit(solution)/shard_map/ppermute | solution.py:32
  29.1 5.0 %collective-permute-start.8 = (bf16[512,128]{1,0:T(8,128)(2,1)S(1)}, bf16[512,128]{1,0:T(8,128)(2,1)S(1)}, u32[]{:S(2)}, u32[]{:S(2)}) collective-permute-start(bf16[512,128]{1,0:T(8,128)(2,1)S(1)} %constant_dynamic-update-slice_fusion.8.refs_0_.refs_4_), channel_id=1, source_target_pairs={{0,64},{64,0},{128,192},{192,128},{1,65},{65,1},{129,193},{193,129... | collective-permute-start | bytes 393224 | tf_op jit(solution)/shard_map/ppermute | solution.py:32
  29.7 8.4 %collective-permute-start.7 = (bf16[2048,128]{1,0:T(8,128)(2,1)S(1)}, bf16[2048,128]{1,0:T(8,128)(2,1)S(1)}, u32[]{:S(2)}, u32[]{:S(2)}) collective-permute-start(bf16[2048,128]{1,0:T(8,128)(2,1)S(1)} %constant_dynamic-update-slice_fusion.25.refs_1_.refs_3_), channel_id=1, source_target_pairs={{0,1},{1,0},{2,3},{3,2},{4,5},{5,4},{6,7},{7,6},{8,9},{9,8},{10,11... | collective-permute-start | bytes 1572872 | tf_op jit(solution)/shard_map/ppermute | solution.py:32
  35.0 6.8 %collective-permute-start.11 = (bf16[1536,128]{1,0:T(8,128)(2,1)S(1)}, bf16[1536,128]{1,0:T(8,128)(2,1)S(1)}, u32[]{:S(2)}, u32[]{:S(2)}) collective-permute-start(bf16[1536,128]{1,0:T(8,128)(2,1)S(1)} %constant_dynamic-update-slice_fusion.36.refs_4_), channel_id=1, source_target_pairs={{0,1},{1,0},{2,3},{3,2},{4,5},{5,4},{6,7},{7,6},{8,9},{9,8},{10,11... | collective-permute-start | bytes 1179656 | tf_op jit(solution)/shard_map/ppermute | solution.py:32
  35.1 1.9 %collective-permute-start.16 = (bf16[512,128]{1,0:T(8,128)(2,1)S(1)}, bf16[512,128]{1,0:T(8,128)(2,1)S(1)}, u32[]{:S(2)}, u32[]{:S(2)}) collective-permute-start(bf16[512,128]{1,0:T(8,128)(2,1)S(1)} %constant_dynamic-update-slice_fusion.8.refs_0_.refs_4_), channel_id=1, source_target_pairs={{0,1},{1,0},{2,3},{3,2},{4,5},{5,4},{6,7},{7,6},{8,9},{9,8},{10,11... | collective-permute-start | bytes 393224 | tf_op jit(solution)/shard_map/ppermute | solution.py:32
  41.8 10.8 %collective-permute-start.12 = (f16[288,128]{1,0:T(8,128)(2,1)S(1)}, f16[288,128]{1,0:T(8,128)(2,1)S(1)}, u32[]{:S(2)}, u32[]{:S(2)}) collective-permute-start(f16[288,128]{1,0:T(8,128)(2,1)S(1)} %convert_element_type.73), channel_id=1, source_target_pairs={{0,64},{64,0},{128,192},{192,128},{1,65},{65,1},{129,193},{193,129... | collective-permute-start | bytes 221192 | tf_op jit(solution)/shard_map/ppermute | solution.py:32
  42.5 11.0 %collective-permute-start.13 = (f16[288,128]{1,0:T(8,128)(2,1)S(1)}, f16[288,128]{1,0:T(8,128)(2,1)S(1)}, u32[]{:S(2)}, u32[]{:S(2)}) collective-permute-start(f16[288,128]{1,0:T(8,128)(2,1)S(1)} %convert_element_type.74), channel_id=1, source_target_pairs={{0,128},{64,192},{128,0},{192,64},{1,129},{65,193},{129,1},{193,65... | collective-permute-start | bytes 221192 | tf_op jit(solution)/shard_map/ppermute | solution.py:32
  45.4 8.2 %collective-permute-start.14 = (f16[288,128]{1,0:T(8,128)(2,1)S(1)}, f16[288,128]{1,0:T(8,128)(2,1)S(1)}, u32[]{:S(2)}, u32[]{:S(2)}) collective-permute-start(f16[288,128]{1,0:T(8,128)(2,1)S(1)} %convert_element_type.75), channel_id=1, source_target_pairs={{0,192},{64,128},{128,64},{192,0},{1,193},{65,129},{129,65},{193,1... | collective-permute-start | bytes 221192 | tf_op jit(solution)/shard_map/ppermute | solution.py:32
  49.3 5.5 %collective-permute-start.19 = (f16[288,128]{1,0:T(8,128)(2,1)S(1)}, f16[288,128]{1,0:T(8,128)(2,1)S(1)}, u32[]{:S(2)}, u32[]{:S(2)}) collective-permute-start(f16[288,128]{1,0:T(8,128)(2,1)S(1)} %convert_element_type.88), channel_id=1, source_target_pairs={{0,12},{4,8},{8,4},{12,0},{1,13},{5,9},{9,5},{13,1},{2,14},{6,10},... | collective-permute-start | bytes 221192 | tf_op jit(solution)/shard_map/ppermute | solution.py:32
  49.9 5.9 %collective-permute-start.18 = (f16[288,128]{1,0:T(8,128)(2,1)S(1)}, f16[288,128]{1,0:T(8,128)(2,1)S(1)}, u32[]{:S(2)}, u32[]{:S(2)}) collective-permute-start(f16[288,128]{1,0:T(8,128)(2,1)S(1)} %convert_element_type.86), channel_id=1, source_target_pairs={{0,8},{4,12},{8,0},{12,4},{1,9},{5,13},{9,1},{13,5},{2,10},{6,14},... | collective-permute-start | bytes 221192 | tf_op jit(solution)/shard_map/ppermute | solution.py:32
  52.7 4.4 %collective-permute-start.17 = (f16[288,128]{1,0:T(8,128)(2,1)S(1)}, f16[288,128]{1,0:T(8,128)(2,1)S(1)}, u32[]{:S(2)}, u32[]{:S(2)}) collective-permute-start(f16[288,128]{1,0:T(8,128)(2,1)S(1)} %convert_element_type.84), channel_id=1, source_target_pairs={{0,4},{4,0},{8,12},{12,8},{1,5},{5,1},{9,13},{13,9},{2,6},{6,2},{1... | collective-permute-start | bytes 221192 | tf_op jit(solution)/shard_map/ppermute | solution.py:32
  53.8 4.0 %collective-permute-start.15 = (f16[144,128]{1,0:T(8,128)(2,1)S(1)}, f16[144,128]{1,0:T(8,128)(2,1)S(1)}, u32[]{:S(2)}, u32[]{:S(2)}) collective-permute-start(f16[144,128]{1,0:T(8,128)(2,1)S(1)} %convert_element_type.80), channel_id=1, source_target_pairs={{0,2},{2,0},{1,3},{3,1},{4,6},{6,4},{5,7},{7,5},{8,10},{10,8},{9,1... | collective-permute-start | bytes 110600 | tf_op jit(solution)/shard_map/ppermute | solution.py:32
  58.2 6.6 %collective-permute-start.22 = (f16[96,128]{1,0:T(8,128)(2,1)S(1)}, f16[96,128]{1,0:T(8,128)(2,1)S(1)}, u32[]{:S(2)}, u32[]{:S(2)}) collective-permute-start(f16[96,128]{1,0:T(8,128)(2,1)S(1)} %convert_element_type.94), channel_id=1, source_target_pairs={{0,48},{16,32},{32,16},{48,0},{1,49},{17,33},{33,17},{49,1},{2,50}... | collective-permute-start | bytes 73736 | tf_op jit(solution)/shard_map/ppermute | solution.py:32
  60.5 7.7 %collective-permute-start.21 = (f16[96,128]{1,0:T(8,128)(2,1)S(1)}, f16[96,128]{1,0:T(8,128)(2,1)S(1)}, u32[]{:S(2)}, u32[]{:S(2)}) collective-permute-start(f16[96,128]{1,0:T(8,128)(2,1)S(1)} %convert_element_type.92), channel_id=1, source_target_pairs={{0,32},{16,48},{32,0},{48,16},{1,33},{17,49},{33,1},{49,17},{2,34}... | collective-permute-start | bytes 73736 | tf_op jit(solution)/shard_map/ppermute | solution.py:32
  63.2 5.0 %collective-permute-start.20 = (f16[96,128]{1,0:T(8,128)(2,1)S(1)}, f16[96,128]{1,0:T(8,128)(2,1)S(1)}, u32[]{:S(2)}, u32[]{:S(2)}) collective-permute-start(f16[96,128]{1,0:T(8,128)(2,1)S(1)} %convert_element_type.90), channel_id=1, source_target_pairs={{0,16},{16,0},{32,48},{48,32},{1,17},{17,1},{33,49},{49,33},{2,18}... | collective-permute-start | bytes 73736 | tf_op jit(solution)/shard_map/ppermute | solution.py:32
